TPU v7x, 32 devices: a whole 2x2x4 slice. The times are simulated.
32 devices in a mesh: clip: 2 (over x), slab: 16 (over z, y, core).
Axes of the slice: x: 2, y: 2, z: 4, core: 2. Of those that a mesh axis runs over, the one named last changes fastest.
Arguments:
- mask_field: float32 [4096, 2048], P(('clip', 'slab')), parts along dimension 0, may hold values from -1.8 to 2.9
- target_print: int32 [4096, 2048], P(('clip', 'slab')), parts along dimension 0, may hold values from 0 to 1
- source_points: int32 [32, 2], P('clip'), parts along dimension 0, may hold values from 0 to 60
- source_groups: int32 [32], P('clip'), parts along dimension 0, may hold values from 0 to 7
- group_logits: float32 [16], P('clip'), parts along dimension 0, may hold values from -1 to 1
- pupil_radius: int32 [2], P('clip'), parts along dimension 0, may hold values from 32 to 127
Outputs:
- loss_value: float32 [2], P('clip'), parts along dimension 0
- mask_grad: float32 [4096, 2048], P(('clip', 'slab')), parts along dimension 0
- group_grad: float32 [16], P('clip'), parts along dimension 0
There are 2 independent parts, one for each index of `clip`. A program takes and returns all parts, laid end to end along the dimension named above; each array names one. Nothing has to cross between parts.
All inputs are finite; a program needn't handle non-finite values.
Results may differ from a plain program's by a relative error of at most 0.0003.
Values sent between devices are 32-bit elements; how exact they have to be, the bound alone decides.
A program may use at most 128 MiB of HBM per device.

v0:
```python
import functools
import math

import jax
import jax.numpy as jnp
import numpy as np
from jax import lax
from jax.sharding import PartitionSpec as P

K = 256
GRID = 61
NG = 8

steepness = 8.0
threshold = 0.3
shift_scale = 45
HIGH = lax.Precision.HIGH


def dot(form, left, right):
    return jnp.einsum(form, left, right, precision=HIGH, preferred_element_type=jnp.float32)


def waves(left, right, length):
    turns = np.mod(np.asarray(left)[:, None] * np.asarray(right)[None, :], length)
    angles = 2.0 * math.pi * turns.astype(np.float64) / length
    return np.cos(angles), np.sin(angles)


def turned(first, second):
    return (
        first[0] * second[0] - first[1] * second[1],
        first[1] * second[0] + first[0] * second[1],
    )


def shifted_waves(count, freq, length, device, devices):
    near = np.stack(waves(np.arange(count), freq, length)).astype(np.float32)
    far = np.stack(waves(np.arange(devices) * count, freq, length)).astype(np.float32)
    far = lax.dynamic_slice_in_dim(jnp.asarray(far), device, 1, axis=1)
    return turned((far[0], far[1]), (jnp.asarray(near[0]), jnp.asarray(near[1])))


def exchange(blocks):
    return lax.all_to_all(blocks, "slab", 0, 0)


def gather(block, devices):
    return lax.all_gather(block, "slab", tiled=True)


def on_device(devices, mask_field, target_print, source_points, source_groups, group_logits, pupil_radius):
    rows, n = mask_field.shape
    sources = source_points.shape[0]
    coarse = 2 * K
    step = n // coarse
    cols = coarse // devices
    half = n // 2
    device = lax.axis_index("slab")
    freq = np.arange(K, dtype=np.int64) - K // 2
    order = np.concatenate([freq[freq % 2 == 0], freq[freq % 2 == 1]])
    kh = K // 2
    norming = 1.0 / (n * n)

    cos_y, sin_y = waves(np.arange(half), order, n)
    fold = [
        jnp.asarray(np.concatenate([t[:, p * kh : (p + 1) * kh] for t in (cos_y, sin_y)], 1), jnp.float32)
        for p in (0, 1)
    ]
    lag = np.mod(np.arange(n)[None, :] - step * np.arange(coarse)[:, None], n)
    kernel = np.zeros(n)
    for f in range(1, K):
        kernel += 2.0 * np.cos(2.0 * math.pi * np.mod(f * np.arange(n), n) / n)
    kernel = (kernel + 1.0) / coarse
    up = jnp.asarray(kernel[lag], jnp.float32)
    cos_c, sin_c = waves(freq, np.arange(coarse), coarse)
    wave_x = jnp.asarray(np.concatenate([cos_c, sin_c], 1), jnp.float32)
    loc_c, loc_s = shifted_waves(rows, freq, n, device, devices)
    loc = jnp.concatenate([loc_c, loc_s], 1)
    a, b = shifted_waves(cols, order, coarse, device, devices)
    lift = jnp.concatenate([jnp.concatenate([a, -b], 1), jnp.concatenate([b, a], 1)], 0)

    cutoff = pupil_radius[0]
    shifted = (source_points - GRID // 2) * cutoff // shift_scale
    first = jnp.asarray(freq, jnp.int32)[None, None, :] + shifted[:, 0, None, None]
    second = jnp.asarray(np.tile(order, 2), jnp.int32)[None, :, None] + shifted[:, 1, None, None]
    passed = first * first + second * second <= cutoff * cutoff

    near, away = mask_field[:, :half], mask_field[:, half:]
    even = dot("xy,yq->xq", near + away, fold[0])
    odd = dot("xy,yq->xq", near - away, fold[1])
    part_c = jnp.concatenate([even[:, :kh], odd[:, :kh]], 1)
    part_s = jnp.concatenate([even[:, kh:], odd[:, kh:]], 1)
    spec = dot("xq,xk->qk", jnp.concatenate([part_c, part_s], 1), loc)
    band = jnp.concatenate(
        [spec[:K, :K] - spec[K:, K:], -(spec[:K, K:] + spec[K:, :K])], 0
    )
    band = jnp.sum(exchange(band.reshape(devices, 2 * K // devices, K)), 0)
    band = gather(band, devices)

    kept = jnp.where(passed, band[None], 0.0)
    wide = dot("aq,sqk->sak", lift, kept)
    both = dot("ak,kx->ax", wide.reshape(sources * 2 * cols, K), wave_x)
    both = both.reshape(sources, 2, cols, 2 * coarse)
    field_re = (both[:, 0, :, :coarse] - both[:, 1, :, coarse:]) * norming
    field_im = (both[:, 0, :, coarse:] + both[:, 1, :, :coarse]) * norming
    bright = field_re * field_re + field_im * field_im
    onehot = (source_groups[:, None] == jnp.arange(NG, dtype=jnp.int32)[None, :]).astype(jnp.float32)
    weights = jnp.exp(jnp.sum(onehot * group_logits[None, :], 1))
    total = jnp.sum(weights)
    share = weights / total
    image = jnp.sum(share[:, None, None] * bright, 0)

    tall = dot("cm,mx->cx", image, up)
    tall = lax.all_to_all(tall, "slab", 1, 0, tiled=True)
    intensity = dot("cx,cy->xy", tall, up)
    resist = jax.nn.sigmoid(steepness * (intensity - threshold))
    misfit = resist - target_print.astype(jnp.float32)
    slope = (2.0 * steepness) * misfit * resist * (1.0 - resist)
    squares = jnp.sum(misfit * misfit)
    down = dot("xy,cy->cx", slope, up)
    down = lax.all_to_all(down, "slab", 0, 1, tiled=True)
    pull = dot("cx,mx->cm", down, up)

    per_source = jnp.sum(bright * pull[None], (1, 2))
    sums = jnp.concatenate([per_source, squares[None]])
    factor = (2.0 * norming) * share[:, None, None] * pull[None]
    back = jnp.stack([factor * field_re, factor * field_im], 1)
    low = dot("ax,kx->ak", back.reshape(sources * 2 * cols, coarse), wave_x[:, :coarse])
    lows = dot("ax,kx->ak", back.reshape(sources * 2 * cols, coarse), wave_x[:, coarse:])
    low = low.reshape(sources, 2, cols, K)
    lows = lows.reshape(sources, 2, cols, K)
    settle = jnp.concatenate([low[:, 0] + lows[:, 1], low[:, 1] - lows[:, 0]], 1)
    settle = dot("aq,sak->sqk", lift, settle)
    grad_band = jnp.sum(jnp.where(passed, settle, 0.0), 0).reshape(devices, 2 * K // devices, K)
    extra = jnp.pad(sums[None, :], ((0, 7), (0, K - sources - 1)))
    extra = jnp.broadcast_to(extra[None], (devices, 8, K))
    grad_band = jnp.sum(exchange(jnp.concatenate([grad_band, extra], 1)), 0)
    sums = grad_band[-8, : sources + 1]
    grad_band = gather(grad_band[:-8], devices)
    per_source, squares = sums[:-1], sums[-1]
    loss_value = (squares * norming).reshape(1)
    against = jnp.sum(share * per_source)
    source_pull = share * (per_source - against)
    group_grad = jnp.sum(onehot * source_pull[:, None], 0) * norming


    loc_c2 = jnp.concatenate([loc_c, loc_s], 0)
    spread = dot("tk,qk->tq", loc_c2, grad_band)
    spread_re = spread[:rows, :K] - spread[rows:, K:]
    spread_im = spread[:rows, K:] + spread[rows:, :K]
    even = dot("xq,yq->xy", jnp.concatenate([spread_re[:, :kh], -spread_im[:, :kh]], 1), fold[0])
    odd = dot("xq,yq->xy", jnp.concatenate([spread_re[:, kh:], -spread_im[:, kh:]], 1), fold[1])
    mask_grad = jnp.concatenate([even + odd, even - odd], 1)
    return loss_value, mask_grad, group_grad


def solution(mesh):
    in_specs = (
        P(("clip", "slab"), None),
        P(("clip", "slab"), None),
        P("clip", None),
        P("clip"),
        P("clip"),
        P("clip"),
    )
    out_specs = (P("clip"), P(("clip", "slab"), None), P("clip"))
    return jax.shard_map(
        functools.partial(on_device, mesh.shape["slab"]),
        mesh=mesh, in_specs=in_specs, out_specs=out_specs, check_vma=False,
    )
```

profile of v0, /device:TPU:0, one launch (start us, length us, event | category | flops | bytes accessed | tf_op | source)
XLA Modules:
  0.0 150.6 jit_solution(6322485100976151592)
XLA Ops:
  0.6 2.0 %fusion.29 = f32[128,256]{1,0:T(8,128)S(1)} fusion(f32[1024,256]{1,0:T(8,128)} %constant.67.clone, f32[128,2048]{1,0:T(8,128)} %param.18), kind=kOutput, calls=%fused_computation.51 | convolution fusion | flops 201457664 | bytes 2228224 | tf_op jit(solution)/shard_map/xy,yq->xq/dot_general | solution.py:21
  2.6 0.0 copy-start.16
  2.6 0.0 copy-start.17
  2.6 0.0 copy-start.15
  2.6 0.0 copy-start.14
  2.7 0.0 copy-start.13
  2.7 0.0 copy-start.11
  2.7 0.0 copy-start.12
  2.7 2.0 %fusion.27 = f32[128,256]{1,0:T(8,128)S(1)} fusion(f32[1024,256]{1,0:T(8,128)} %constant.68.clone, f32[128,2048]{1,0:T(8,128)} %param.18), kind=kOutput, calls=%fused_computation.49 | convolution fusion | flops 201457664 | bytes 2228224 | tf_op jit(solution)/shard_map/xy,yq->xq/dot_general | solution.py:21
  4.7 0.8 constant_dynamic-slice_fusion
  5.5 1.0 multiply_subtract_fusion
  6.5 0.6 fusion.37
  7.1 0.1 slice_subtract_fusion.2
  7.2 0.8 pad_maximum_fusion.5
  8.0 7.4 %all-to-all-start = ((f32[16,32,256]{2,1,0:T(8,128)}), f32[16,32,256]{2,1,0:T(8,128)S(1)}, u32[]{:S(2)}, u32[]{:S(2)}) async-start(f32[16,32,256]{2,1,0:T(8,128)} %bitcast.5), calls=%async_computation | async-start | bytes 1048576 | tf_op jit(solution)/shard_map/all_to_all | solution.py:45
  16.1 0.1 select_reduce_fusion.1
  16.2 0.6 exponential_reduce_fusion
  16.8 0.7 broadcast_multiply_fusion.1
  17.5 0.1 add_multiply_fusion.1
  17.6 0.1 add_multiply_fusion
  17.7 12.0 %all-to-all-done = f32[16,32,256]{2,1,0:T(8,128)S(1)} async-done(((f32[16,32,256]{2,1,0:T(8,128)}), f32[16,32,256]{2,1,0:T(8,128)S(1)}, u32[]{:S(2)}, u32[]{:S(2)}) %all-to-all-start) | async-done | bytes 524320 | tf_op jit(solution)/shard_map/all_to_all | solution.py:45
  29.7 21.3 %all_gather.6 = f32[512,256]{1,0:T(8,128)S(1)} all-gather(f32[32,256]{1,0:T(8,128)S(1)} %reduce_sum.92), channel_id=1, replica_groups=mesh['clip'=2,'slab'=16] {'slab'}, dimensions={0}, use_global_device_ids=true | all-gather | bytes 557056 | tf_op jit(solution)/shard_map/all_gather | solution.py:49
  51.1 0.2 copy.43
  51.3 0.0 copy-start.4
  51.3 4.5 %fusion.1 = f32[16,256,64]{1,2,0:T(8,128)S(1)} fusion(f32[512,256]{0,1:T(8,128)S(1)} %copy.43, s32[]{:T(128)S(6)} %mul.218, s32[16,512]{1,0:T(8,128)S(1)} %add_multiply_fusion, s32[16,256]{1,0:T(8,128)S(1)} %add_multiply_fusion.1, f32[32,256]{1,0:T(8,128)S(1)} %get-tuple-element.21, f32[32,256]{1,0:T(8,128)S(1)} %get-tuple-element.20, ...), kind=kOutput, calls=%fused_computation.2 | convolution fusion | flops 811696128 | bytes 1720324 | tf_op jit(solution)/shard_map/aq,sqk->sak/dot_general | solution.py:21
  55.7 0.0 copy-start.1
  55.7 1.9 %fusion.72 = f32[16,2,32,1024]{3,2,1,0:T(8,128)S(1)} fusion(f32[16,2,32,256]{3,2,1,0:T(8,128)S(1)} %bitcast.96, f32[256,1024,1,1]{1,0,3,2:T(8,128)S(1)} %copy-done.4), kind=kOutput, calls=%fused_computation.126 | convolution fusion | flops 1610612736 | bytes 6291456 | tf_op jit(solution)/shard_map/ak,kx->ax/dot_general | solution.py:21
  57.6 0.0 copy-start.3
  57.6 0.5 fusion.20
  58.2 2.0 %fusion.57 = f32[32,16,128]{2,0,1:T(8,128)S(1)} fusion(f32[16,128,512]{2,1,0:T(8,128)S(1)} %copy-done.1, f32[32,512]{1,0:T(8,128)S(1)} %fusion.20), kind=kOutput, calls=%fused_computation.89 | convolution fusion | flops 201326592 | bytes 4521984 | tf_op jit(solution)/shard_map/cm,mx->cx/dot_general | solution.py:21
  60.2 0.0 copy-start
  60.2 12.9 %all_to_all.45 = f32[32,16,128]{2,0,1:T(8,128)S(1)} all-to-all(f32[32,16,128]{2,0,1:T(8,128)S(1)} %fusion.57), channel_id=1, replica_groups=mesh['clip'=2,'slab'=16] {'slab'}, dimensions={1} | all-to-all | bytes 524288 | tf_op jit(solution)/shard_map/all_to_all | solution.py:115
  73.1 0.2 copy.45
  73.3 2.4 %multiply_reduce_fusion = (f32[]{:T(128)}, f32[128,2048]{1,0:T(8,128)S(1)}) fusion(s32[128,2048]{1,0:T(8,128)S(1)} %copy-done.2, f32[512,128]{1,0:T(8,128)S(1)} %bitcast.97, f32[512,2048]{1,0:T(8,128)S(1)} %copy-done.3), kind=kOutput, calls=%fused_computation.35 | convolution fusion | flops 807665664 | bytes 6553604 | tf_op jit(solution)/shard_map/cx,cy->xy/dot_general | solution.py:21
  75.7 1.9 %fusion.22 = f32[512,128]{1,0:T(8,128)S(1)} fusion(f32[512,2048]{1,0:T(8,128)S(1)} %copy-done, f32[128,2048]{1,0:T(8,128)S(1)} %get-tuple-element.29, s32[128,2048]{1,0:T(8,128)S(1)} %copy-done.2), kind=kOutput, calls=%fused_computation.39 | convolution fusion | flops 806879232 | bytes 6553600 | tf_op jit(solution)/shard_map/xy,cy->cx/dot_general | solution.py:21
  77.6 12.8 %all_to_all.46 = f32[16,32,128]{2,1,0:T(8,128)S(1)} all-to-all(f32[16,32,128]{2,1,0:T(8,128)S(1)} %bitcast.95), channel_id=1, replica_groups=mesh['clip'=2,'slab'=16] {'slab'}, dimensions={0} | all-to-all | bytes 524288 | tf_op jit(solution)/shard_map/all_to_all | solution.py:122
  90.3 2.0 %fusion.52 = f32[32,512]{1,0:T(8,128)S(1)} fusion(f32[512,2048]{1,0:T(8,128)S(1)} %copy-done, f32[16,32,128]{2,1,0:T(8,128)S(1)} %all_to_all.46), kind=kOutput, calls=%fused_computation.77 | convolution fusion | flops 201326592 | bytes 4521984 | tf_op jit(solution)/shard_map/cx,mx->cm/dot_general | solution.py:21
  92.4 0.4 fusion.21
  92.8 0.6 multiply_multiply_fusion.1
  93.4 0.4 copy-done.7
  93.8 1.0 fusion.13
  94.9 1.0 fusion.14
  95.9 0.1 fusion.23
  96.0 0.1 fusion.25
  96.1 0.7 maximum_bitcast_fusion.3
  96.8 4.5 %fusion = f32[512,256]{0,1:T(8,128)S(1)} fusion(s32[]{:T(128)S(6)} %mul.218, s32[16,512]{1,0:T(8,128)S(1)} %add_multiply_fusion, s32[16,256]{1,0:T(8,128)S(1)} %add_multiply_fusion.1, f32[16,32,256]{2,1,0:T(8,128)S(1)} %fusion.23, f32[16,32,256]{2,1,0:T(8,128)S(1)} %fusion.25, f32[32,256]{1,0:T(8,128)S(1)} %get-tuple-element.21, ...), kind=kOutput, calls=%fused_computation.1 | convolution fusion | flops 813924352 | bytes 1720324 | tf_op jit(solution)/shard_map/aq,sak->sqk/dot_general | solution.py:21
  101.4 0.0 copy-start.9
  101.4 0.0 copy-start.8
  101.4 0.2 copy.49
  101.6 0.0 copy-start.5
  101.7 0.0 copy-start.10
  101.7 21.1 %all_to_all.47 = f32[16,40,256]{2,1,0:T(8,128)S(1)} all-to-all(f32[16,40,256]{2,1,0:T(8,128)S(1)} %pad_maximum_fusion.4), channel_id=1, replica_groups=mesh['clip'=2,'slab'=16] {'slab'}, dimensions={0} | all-to-all | bytes 1310720 | tf_op jit(solution)/shard_map/all_to_all | solution.py:45
  122.8 0.6 multiply_reduce_fusion.1
  123.4 0.6 slice.179
  124.0 0.6 subtract_multiply_fusion.2
  124.7 0.1 select_reduce_fusion
  124.8 0.5 broadcast_multiply_fusion
  125.3 20.4 %all_gather.7 = f32[512,256]{1,0:T(8,128)S(1)} all-gather(f32[32,256]{1,0:T(8,128)S(1)} %slice.180), channel_id=1, replica_groups=mesh['clip'=2,'slab'=16] {'slab'}, dimensions={0}, use_global_device_ids=true | all-gather | bytes 557056 | tf_op jit(solution)/shard_map/all_gather | solution.py:49
  145.7 0.4 fusion.48
  146.2 0.4 fusion.53
  146.6 0.4 fusion.55
  147.6 0.4 convolution_add_fusion.1
  148.0 0.4 fusion.69
  148.5 1.0 pad_maximum_fusion.3
  (31 shorter events, 0.3 us)
Async XLA Ops:
  2.6 13.5 %copy-start.16 = (f32[8]{0:T(128)S(1)}, f32[8]{0:T(128)}, u32[]{:S(2)}) copy-start(f32[8]{0:T(128)} %param.22) | copy-start | bytes 100
  2.6 13.5 %copy-start.17 = (s32[16]{0:T(128)S(1)}, s32[16]{0:T(128)}, u32[]{:S(2)}) copy-start(s32[16]{0:T(128)} %param.21) | copy-start | bytes 196
  2.6 14.2 %copy-start.15 = (s32[16,2]{0,1:T(2,128)S(1)}, s32[16,2]{0,1:T(2,128)}, u32[]{:S(2)}) copy-start(s32[16,2]{0,1:T(2,128)} %param.20) | copy-start | bytes 388
  2.6 14.8 %copy-start.14 = (s32[256]{0:T(256)S(1)}, s32[256]{0:T(256)}, u32[]{:S(2)}) copy-start(s32[256]{0:T(256)} %constant.77.clone) | copy-start | bytes 3076
  2.7 14.9 %copy-start.13 = (s32[512]{0:T(512)S(1)}, s32[512]{0:T(512)}, u32[]{:S(2)}) copy-start(s32[512]{0:T(512)} %constant.78.clone) | copy-start | bytes 6148
  2.7 15.0 %copy-start.11 = (f32[32,256]{1,0:T(8,128)S(1)}, f32[32,256]{1,0:T(8,128)}, u32[]{:S(2)}) copy-start(f32[32,256]{1,0:T(8,128)} %constant.76.clone) | copy-start | bytes 98308
  2.7 15.0 %copy-start.12 = (f32[32,256]{1,0:T(8,128)S(1)}, f32[32,256]{1,0:T(8,128)}, u32[]{:S(2)}) copy-start(f32[32,256]{1,0:T(8,128)} %constant.75.clone) | copy-start | bytes 98308
  8.0 21.7 %all-to-all-start = ((f32[16,32,256]{2,1,0:T(8,128)}), f32[16,32,256]{2,1,0:T(8,128)S(1)}, u32[]{:S(2)}, u32[]{:S(2)}) async-start(f32[16,32,256]{2,1,0:T(8,128)} %bitcast.5), calls=%async_computation | async-start | bytes 1048576 | tf_op jit(solution)/shard_map/all_to_all | solution.py:45
  51.3 4.5 %copy-start.4 = (f32[256,1024,1,1]{1,0,3,2:T(8,128)S(1)}, f32[256,1024,1,1]{1,0,3,2:T(8,128)}, u32[]{:S(2)}) copy-start(f32[256,1024,1,1]{1,0,3,2:T(8,128)} %constant.93) | copy-start | bytes 3145732
  55.7 2.5 %copy-start.1 = (f32[16,128,512]{2,1,0:T(8,128)S(1)}, f32[16,128,512]{2,1,0:T(8,128)}, u32[]{:S(2)}) copy-start(f32[16,128,512]{2,1,0:T(8,128)} %constant.83) | copy-start | bytes 12582916
  57.6 15.6 %copy-start.2 = (s32[128,2048]{1,0:T(8,128)S(1)}, s32[128,2048]{1,0:T(8,128)}, u32[]{:S(2)}) copy-start(s32[128,2048]{1,0:T(8,128)} %param.19) | copy-start | bytes 3145732
  57.6 15.6 %copy-start.3 = (f32[512,2048]{1,0:T(8,128)S(1)}, f32[512,2048]{1,0:T(8,128)}, u32[]{:S(2)}) copy-start(f32[512,2048]{1,0:T(8,128)} %constant.86) | copy-start | bytes 12582916
  60.2 15.5 %copy-start = (f32[512,2048]{1,0:T(8,128)S(1)}, f32[512,2048]{1,0:T(8,128)}, u32[]{:S(2)}) copy-start(f32[512,2048]{1,0:T(8,128)} %constant.69.clone) | copy-start | bytes 12582916
  92.8 1.0 copy-start.7
  92.8 2.1 %copy-start.6 = (f32[256,512,1,1]{1,0,3,2:T(8,128)S(1)}, f32[256,512,1,1]{1,0,3,2:T(8,128)}, u32[]{:S(2)}) copy-start(f32[256,512,1,1]{1,0,3,2:T(8,128)} %constant.94) | copy-start | bytes 1572868
  101.4 44.8 %copy-start.9 = (f32[1024,128]{1,0:T(8,128)S(1)}, f32[1024,128]{1,0:T(8,128)}, u32[]{:S(2)}) copy-start(f32[1024,128]{1,0:T(8,128)} %constant.91) | copy-start | bytes 1572868
  101.4 45.2 %copy-start.8 = (f32[1024,128]{1,0:T(8,128)S(1)}, f32[1024,128]{1,0:T(8,128)}, u32[]{:S(2)}) copy-start(f32[1024,128]{1,0:T(8,128)} %constant.89) | copy-start | bytes 1572868
  101.6 46.0 %copy-start.5 = (f32[1024,128]{1,0:T(8,128)S(1)}, f32[1024,128]{1,0:T(8,128)}, u32[]{:S(2)}) copy-start(f32[1024,128]{1,0:T(8,128)} %constant.92) | copy-start | bytes 1572868
  101.7 46.4 %copy-start.10 = (f32[1024,128]{1,0:T(8,128)S(1)}, f32[1024,128]{1,0:T(8,128)}, u32[]{:S(2)}) copy-start(f32[1024,128]{1,0:T(8,128)} %constant.90) | copy-start | bytes 1572868
where the time goes:
time: 151 us
  blocking collectives  88.5 us (59%)
  matrix products  27.8 us (18%)
  waiting for transfers between devices  12 us (8%)
  other arithmetic  8.98 us (6%)
  starting transfers between devices  7.41 us (5%)
  between operations  3.55 us (2%)
  local copies, waits for them, and re-layouts  2.46 us (2%)
    all_gather x2, blocking collectives, gather(): return lax.all_gather(block, 'slab', tiled=True)  41.7 us
    dot_general x17, matrix products, dot(): jnp.einsum(form, left, right, precision=HIGH, preferred_element_type=jnp....  27.8 us
    all_to_all x1, blocking collectives, exchange(): return lax.all_to_all(blocks, 'slab', 0, 0)  21.1 us
    all_to_all x1, blocking collectives, on_device(): tall = lax.all_to_all(tall, 'slab', 1, 0, tiled=True)  12.9 us
    all_to_all x1, blocking collectives, on_device(): down = lax.all_to_all(down, 'slab', 0, 1, tiled=True)  12.8 us
    all_to_all x1, waiting for transfers between devices, exchange(): return lax.all_to_all(blocks, 'slab', 0, 0)  12 us
    all_to_all x1, starting transfers between devices, exchange(): return lax.all_to_all(blocks, 'slab', 0, 0)  7.41 us
  transfers between devices with their start and end apart: 1, of which 1 were waited for; matrix products, arithmetic and copies ran while one was open for 1% of the time, Pallas kernels for 0%

commit v1 on v0

v1 whole, which is shorter than its diff:
```python
import functools
import math

import jax
import jax.numpy as jnp
import numpy as np
from jax import lax
from jax.experimental import pallas as pl
from jax.experimental.pallas import tpu as pltpu
from jax.sharding import PartitionSpec as P

K = 256
GRID = 61
NG = 8

steepness = 8.0
threshold = 0.3
shift_scale = 45
F32 = jnp.float32
BF16 = jnp.bfloat16
LANES = 128
SUB = 8


def angles(left, right, length):
    turns = np.mod(np.asarray(left)[:, None] * np.asarray(right)[None, :], length)
    return 2.0 * math.pi * turns.astype(np.float64) / length


def halves(table):
    table = np.asarray(table, np.float32)
    high = table.astype(BF16)
    low = (table - high.astype(np.float32)).astype(BF16)
    return np.stack([high, low])


def split(value):
    high = value.astype(BF16)
    return high, (value - high.astype(F32)).astype(BF16)


def product(left, right, flip=False):
    dims = (((1,), (1 if flip else 0,)), ((), ()))
    one = lambda a, b: lax.dot_general(a, b, dims, preferred_element_type=F32)
    return one(left[0], right[0]) + one(left[1], right[0]) + one(left[0], right[1])


def tables(n, rows, devices):
    h = K // 2
    coarse = 2 * K
    step = n // coarse
    freq = np.arange(h)
    near = np.arange(rows)
    wave_y = angles(freq, np.arange(n), n)
    wave_y = np.concatenate([np.cos(wave_y), np.sin(wave_y)], 0)
    wave_x = angles(near, freq, n)
    wave_x = np.concatenate([np.cos(wave_x), np.sin(wave_x)], 1)
    half_x = angles(near, 2 * freq + 1, 2 * n)
    half_x = np.concatenate([np.cos(half_x), -np.sin(half_x)], 1)
    half_y = angles(2 * freq + 1, step * np.arange(coarse), 2 * n)
    half_y = np.concatenate([np.cos(half_y), np.sin(half_y)], 0)
    far = angles(rows * np.arange(devices), freq, n)
    far = np.stack([np.cos(far), np.sin(far)])[:, :, None, :].astype(np.float32)
    half_far = angles(rows * np.arange(devices), 2 * freq + 1, 2 * n)
    half_far = np.stack([np.cos(half_far), np.sin(half_far)]) / (n * n)
    half_far = half_far[:, :, None, :].astype(np.float32)
    block = 2 * LANES
    extra = n // step - block // step
    lag = np.mod(np.arange(block)[None, :] - step * (np.arange(coarse + extra) - extra)[:, None], n)
    kernel = np.ones(n)
    for f in range(1, K):
        kernel += 2.0 * np.cos(2.0 * math.pi * np.mod(f * np.arange(n), n) / n)
    up = (kernel / coarse)[lag]
    edge = angles([h], np.arange(LANES), n)
    edge = np.concatenate([np.cos(edge), np.sin(edge)], 0)
    edge = np.concatenate([edge, np.zeros((SUB - 2, LANES))], 0)
    return {
        "wave_y": halves(wave_y),
        "wave_x": halves(wave_x),
        "half_x": halves(half_x),
        "half_xt": halves(half_x.T),
        "half_y": halves(half_y),
        "half_yt": halves(half_y.T),
        "up": halves(up),
        "far": far,
        "half_far": half_far,
        "edge": edge.astype(np.float32),
    }


NAMES = ("wave_y", "wave_x", "half_x", "half_xt", "half_y", "half_yt", "up", "far", "half_far", "edge")


def kernel(devices, n, *refs):
    points, groups, logits, radius, mask_hbm, target_hbm = refs[:6]
    sources_in = dict(zip(NAMES, refs[6 : 6 + len(NAMES)]))
    refs = refs[6 + len(NAMES) :]
    loss_ref, grad_hbm, group_ref = refs[:3]
    refs = refs[3:]
    tab = dict(zip(NAMES, refs[: len(NAMES)]))
    refs = refs[len(NAMES) :]
    (mask, target, rows_t, edge_out, rows_in, edge_in, chunk, edge_all, ext, band, data, fields, image, pull,
     grads, grad_t, edge_back, grad_in, edge_back_in, edge_back_all, back_rows, back_in, spread, out,
     local_sem, out_sem, send_sem, recv_sem) = refs
    h = K // 2
    coarse = 2 * K
    sources = points.shape[0]
    rows = mask.shape[0]
    block = 2 * LANES
    blocks = n // block
    step = n // coarse
    me = lax.axis_index("slab")
    norming = 1.0 / (n * n)

    loads = {}
    for i, (name, src, dst) in enumerate(
        [("mask", mask_hbm, mask), ("wave_y", sources_in["wave_y"], tab["wave_y"])]
        + [(k, sources_in[k], tab[k]) for k in ("edge", "wave_x", "far", "half_far", "half_x", "half_y")]
        + [("up", sources_in["up"], tab["up"]), ("target", target_hbm, target)]
        + [(k, sources_in[k], tab[k]) for k in ("half_yt", "half_xt")]
    ):
        loads[name] = pltpu.make_async_copy(src, dst, local_sem.at[i])
        loads[name].start()

    barrier = pltpu.get_barrier_semaphore()

    def greet(i, carry):
        pl.semaphore_signal(barrier, inc=1, device_id={"slab": lax.rem(me + i, devices)})
        return carry

    lax.fori_loop(1, devices, greet, 0)

    def both(name):
        return tab[name][0], tab[name][1]

    def copy_to(phase, peer, src, dst):
        return pltpu.make_async_remote_copy(
            src_ref=src, dst_ref=dst, send_sem=send_sem.at[phase, peer], recv_sem=recv_sem.at[phase, me],
            device_id={"slab": peer},
        )

    def send_all(phase, src_of, dst):
        def body(i, carry):
            peer = lax.rem(me + i, devices)
            copy_to(phase, peer, src_of(peer), dst).start()
            return carry

        lax.fori_loop(1, devices, body, 0)

    def wait_all(phase, src, dst_of):
        def body(i, carry):
            peer = lax.rem(me + i, devices)
            pltpu.make_async_remote_copy(
                src_ref=src, dst_ref=dst_of(peer), send_sem=send_sem.at[phase, peer],
                recv_sem=recv_sem.at[phase, peer], device_id={"slab": peer},
            ).wait_recv()
            return carry

        lax.fori_loop(1, devices, body, 0)

    def drain(phase, src, dst):
        def body(i, carry):
            peer = lax.rem(me + i, devices)
            copy_to(phase, peer, src, dst).wait_send()
            return carry

        lax.fori_loop(1, devices, body, 0)

    lane = lax.broadcasted_iota(jnp.int32, (1, LANES), 1)

    def column(row):
        return jnp.broadcast_to(row, (LANES, LANES)).T

    logit_row = jnp.full((1, LANES), 0.0, F32)
    group_row = jnp.full((1, LANES), -1, jnp.int32)
    for s in range(sources):
        g = groups[s]
        logit_row = jnp.where(lane == s, logits[g], logit_row)
        group_row = jnp.where(lane == s, g, group_row)
    weight_row = jnp.where(lane < sources, jnp.exp(logit_row), 0.0)
    share_row = weight_row / jnp.sum(weight_row, axis=1, keepdims=True)

    loads["mask"].wait()
    loads["wave_y"].wait()
    transformed = product(split(mask[...]), both("wave_y"), flip=True)
    rows_t[0] = transformed[:, :h].T
    rows_t[1] = transformed[:, h:].T
    loads["edge"].wait()
    loads["wave_x"].wait()
    loads["far"].wait()
    edge_rows = tab["edge"][...]
    edge_pair = split(edge_rows)
    summed = mask[:, :LANES]
    for b in range(1, n // LANES):
        summed = summed + mask[:, b * LANES : (b + 1) * LANES]
    side_x = product(edge_pair, split(transformed))
    last = product(edge_pair, split(summed), flip=True)
    side_y = product(split(last), both("wave_x"))
    far_c, far_s = tab["far"][0, me], tab["far"][1, me]
    side_c = far_c * side_y[:2, :h] - far_s * side_y[:2, h:]
    side_s = far_s * side_y[:2, :h] + far_c * side_y[:2, h:]

    def mixes(cc, cs, sc, ss):
        return cc - ss, cc + ss, sc + cs, sc - cs

    edges = mixes(side_x[0:1, :h], side_x[0:1, h:], side_x[1:2, :h], side_x[1:2, h:])
    edges = edges + mixes(side_c[0:1], side_c[1:2], side_s[0:1], side_s[1:2])

    def lane_sum(value):
        return jnp.sum(value, axis=1, keepdims=True)

    corner = mixes(
        lane_sum(last[0:1] * edge_rows[0:1]), lane_sum(last[1:2] * edge_rows[0:1]),
        lane_sum(last[0:1] * edge_rows[1:2]), lane_sum(last[1:2] * edge_rows[1:2]),
    )
    corner_row = jnp.zeros((1, LANES), F32)
    for i in range(4):
        corner_row = jnp.where(lane == i, corner[i], corner_row)
    for i in range(8):
        edge_out[i] = edges[i]
    edge_out[8] = corner_row
    for i in range(9, devices):
        edge_out[i] = jnp.zeros((1, LANES), F32)

    pl.semaphore_wait(barrier, devices - 1)
    send_all(0, lambda p: rows_t.at[:, pl.ds(p * SUB, SUB), :], rows_in.at[me])
    send_all(1, lambda p: edge_out.at[p], edge_in.at[me])
    rows_in[me] = rows_t[:, pl.ds(me * SUB, SUB), :]
    edge_in[me] = edge_out[me]

    wait_all(0, rows_t.at[:, pl.ds(0, SUB), :], lambda p: rows_in.at[p])
    gathered = rows_in[...].reshape(devices * 2 * SUB, rows)
    turned = product(split(gathered), both("wave_x")).reshape(devices, 2 * SUB, 2 * h)
    far_c, far_s = tab["far"][0], tab["far"][1]
    turned_c, turned_s = turned[:, :, :h], turned[:, :, h:]
    sum_c = jnp.sum(far_c * turned_c - far_s * turned_s, 0)
    sum_s = jnp.sum(far_s * turned_c + far_c * turned_s, 0)
    for i, value in enumerate(mixes(sum_c[:SUB], sum_c[SUB:], sum_s[:SUB], sum_s[SUB:])):
        chunk[me, i] = value
    send_all(2, lambda p: chunk.at[me], chunk.at[me])
    wait_all(1, edge_out.at[0], lambda p: edge_in.at[p])
    edge_all[me] = jnp.sum(edge_in[...], 0)
    send_all(3, lambda p: edge_all.at[me], edge_all.at[me])

    loads["half_far"].wait()
    loads["half_x"].wait()
    loads["half_y"].wait()
    turn_c = column(tab["half_far"][0, me])
    turn_s = column(tab["half_far"][1, me])

    wait_all(2, chunk.at[me], lambda p: chunk.at[p])
    wait_all(3, edge_all.at[me], lambda p: edge_all.at[p])
    shifted = []
    plain = []
    for i in range(4):
        ext[:h, :h] = chunk[:, i].reshape(h, h).T
        ext[h : h + 1, :h] = edge_all[i]
        ext[:h, h:] = column(edge_all[4 + i])
        ext[h : h + 1, h:] = jnp.broadcast_to(lane_sum(jnp.where(lane == i, edge_all[8], 0.0)), (1, LANES))
        plain = ext[...]
        moved = pltpu.roll(plain, 2 * h - 1, 1)
        if i in (0, 2):
            first, second = ext[:h, :h], None
            ext[...] = moved
            second = ext[1 : h + 1, :h]
        else:
            second = ext[1 : h + 1, :h]
            ext[...] = moved
            first = ext[:h, :h]
        data[i, 0] = first
        data[i, 1] = second

    def turn(slot, re, im, sign):
        s = turn_s if sign > 0 else -turn_s
        band[slot, 0] = re * turn_c - im * s
        band[slot, 1] = re * s + im * turn_c

    turn(0, data[0, 0], -data[2, 0], 1)
    turn(1, data[1, 0], -data[3, 0], 1)
    turn(2, data[1, 1], data[3, 1], -1)
    turn(3, data[0, 1], data[2, 1], -1)

    cutoff = radius[0]
    limit = (cutoff * cutoff).astype(F32)
    row_index = lax.broadcasted_iota(jnp.int32, (h, h), 0).astype(F32)
    lane_index = lane.astype(F32)

    def masks(s):
        first = ((points[s, 0] - GRID // 2) * cutoff // shift_scale).astype(F32)
        second = ((points[s, 1] - GRID // 2) * cutoff // shift_scale).astype(F32)
        row_p, row_m = row_index + first, first - 1.0 - row_index
        col_p, col_m = lane_index + second, second - 1.0 - lane_index
        room_p, room_m = limit - row_p * row_p, limit - row_m * row_m
        col_p, col_m = col_p * col_p, col_m * col_m
        return col_p <= room_p, col_m <= room_p, col_p <= room_m, col_m <= room_m

    def share_of(s):
        return lane_sum(jnp.where(lane == s, share_row, 0.0))

    image[...] = jnp.zeros_like(image)

    def forward(s, carry):
        kept = masks(s)
        quads = []
        for part in range(2):
            pp, pm, mp, mm = (jnp.where(kept[q], band[q, part], 0.0) for q in range(4))
            ep, op, em, om = pp + mp, pp - mp, pm + mm, pm - mm
            quads.append((ep + em, ep - em, op + om, op - om))
        (ee_r, eo_r, oe_r, oo_r), (ee_i, eo_i, oe_i, oo_i) = quads
        top = jnp.concatenate([ee_r, -eo_i, ee_i, eo_r], 1)
        low = jnp.concatenate([oe_i, oo_r, -oe_r, oo_i], 1)
        wide = product(both("half_x"), split(jnp.concatenate([top, low], 0)))
        wide = jnp.concatenate([wide[:, : 2 * h], wide[:, 2 * h :]], 0)
        field = product(split(wide), both("half_y"))
        fields[s] = field
        re, im = field[:rows], field[rows:]
        image[...] += share_of(s) * (re * re + im * im)
        return carry

    lax.fori_loop(0, sources, forward, 0)

    loads["up"].wait()
    loads["target"].wait()
    pull[...] = jnp.zeros_like(pull)
    squares = jnp.zeros((rows, LANES), F32)
    image_pair = split(image[...])
    extra = (n - block) // step
    for b in range(blocks):
        start = extra - b * (block // step)
        up = (tab["up"][0, start : start + coarse, :], tab["up"][1, start : start + coarse, :])
        intensity = product(image_pair, up)
        resist = 1.0 / (1.0 + jnp.exp(-steepness * (intensity - threshold)))
        misfit = resist - target[:, b * block : (b + 1) * block].astype(F32)
        slope = (2.0 * steepness) * misfit * resist * (1.0 - resist)
        square = misfit * misfit
        squares = squares + square[:, :LANES] + square[:, LANES:]
        pull[...] += product(split(slope), up, flip=True)
    squares = lane_sum(jnp.sum(squares, 0, keepdims=True))

    loads["half_yt"].wait()
    loads["half_xt"].wait()
    grads[...] = jnp.zeros_like(grads)

    def backward(s, sums):
        kept = masks(s)
        re, im = fields[s, :rows], fields[s, rows:]
        weak = pull[...]
        down_r, down_i = weak * re, weak * im
        total = lane_sum(jnp.sum(down_r * re + down_i * im, 0, keepdims=True))
        sums = jnp.where(lane == s, total, sums)
        scale = 2.0 * share_of(s)
        back = jnp.concatenate([down_r, down_i], 0)
        settle = product(split(back), both("half_yt")) * scale
        settle = jnp.concatenate([settle[:rows], settle[rows:]], 1)
        full = product(both("half_xt"), split(settle))
        ee_r, eo_i, ee_i, eo_r = full[:h, :h], -full[:h, h : 2 * h], full[:h, 2 * h : 3 * h], full[:h, 3 * h :]
        oe_i, oo_r, oe_r, oo_i = full[h:, :h], full[h:, h : 2 * h], -full[h:, 2 * h : 3 * h], full[h:, 3 * h :]
        for part, (ee, eo, oe, oo) in enumerate(((ee_r, eo_r, oe_r, oo_r), (ee_i, eo_i, oe_i, oo_i))):
            ep, em, op, om = ee + eo, ee - eo, oe + oo, oe - oo
            for q, value in enumerate((ep + op, em + om, ep - op, em - om)):
                grads[q, part] += jnp.where(kept[q], value, 0.0)
        return sums

    sums = lax.fori_loop(0, sources, backward, jnp.zeros((1, LANES), F32))
    sums = jnp.where(lane == sources, squares, sums)

    def unturn(slot, sign):
        s = turn_s if sign > 0 else -turn_s
        re, im = grads[slot, 0], grads[slot, 1]
        return re * turn_c + im * s, im * turn_c - re * s

    pp, pm, mp, mm = unturn(0, 1), unturn(1, 1), unturn(2, -1), unturn(3, -1)
    pieces = ((pp[0], mm[0]), (pm[0], mp[0]), (-pp[1], mm[1]), (-pm[1], mp[1]))
    last_row = jnp.zeros((1, LANES), F32)
    for i, (first, second) in enumerate(pieces):
        ext[...] = jnp.zeros_like(ext)
        if i in (0, 2):
            ext[1 : h + 1, :h] = second
            moved = pltpu.roll(ext[...], 1, 1)
            ext[...] = moved
            ext[:h, :h] += first
        else:
            ext[:h, :h] = first
            moved = pltpu.roll(ext[...], 1, 1)
            ext[...] = moved
            ext[1 : h + 1, :h] += second
        grad_t[i] = ext[:h, :h].T
        edge_back[i] = ext[h : h + 1, :h]
        edge_back[4 + i] = ext[:h, h:].T[0:1, :]
        last_row = jnp.where(lane == i, ext[h : h + 1, h : h + 1], last_row)
    edge_back[8] = last_row
    edge_back[9] = sums
    for i in range(10, devices):
        edge_back[i] = jnp.zeros((1, LANES), F32)

    send_all(4, lambda p: grad_t.at[:, pl.ds(p * SUB, SUB), :], grad_in.at[me])
    send_all(5, lambda p: edge_back.at[p], edge_back_in.at[me])
    grad_in[me] = grad_t[:, pl.ds(me * SUB, SUB), :]
    edge_back_in[me] = edge_back[me]
    wait_all(4, grad_t.at[:, pl.ds(0, SUB), :], lambda p: grad_in.at[p])

    def unmix(u, v, wp, wm):
        return u + v, wp - wm, wp + wm, v - u

    mine = jnp.sum(grad_in[...], 0)
    cc, cs, sc, ss = unmix(mine[0], mine[1], mine[2], mine[3])
    sum_c = jnp.concatenate([cc, cs], 0)[None]
    sum_s = jnp.concatenate([sc, ss], 0)[None]
    back_c = far_c * sum_c + far_s * sum_s
    back_s = far_c * sum_s - far_s * sum_c
    turned = jnp.concatenate([back_c, back_s], 2).reshape(devices * 2 * SUB, 2 * h)
    gathered = product(split(turned), both("wave_x"), flip=True)
    back_rows[...] = gathered.reshape(devices, 2, SUB, rows)
    send_all(6, lambda p: back_rows.at[p], back_in.at[:, pl.ds(me * SUB, SUB), :])
    back_in[:, pl.ds(me * SUB, SUB), :] = back_rows[me]
    wait_all(5, edge_back.at[0], lambda p: edge_back_in.at[p])
    edge_back_all[me] = jnp.sum(edge_back_in[...], 0)
    send_all(7, lambda p: edge_back_all.at[me], edge_back_all.at[me])
    wait_all(7, edge_back_all.at[me], lambda p: edge_back_all.at[p])

    sums = edge_back_all[9]
    loss_ref[0] = jnp.sum(jnp.where(lane == sources, sums, 0.0)) * norming
    sums = jnp.where(lane < sources, sums, 0.0)
    source_pull = share_row * (sums - lane_sum(share_row * sums))
    for g in range(NG):
        group_ref[g] = jnp.sum(jnp.where(group_row == g, source_pull, 0.0)) * norming

    side_x = unmix(*(edge_back_all[i] for i in range(4)))
    side_y = unmix(*(edge_back_all[4 + i] for i in range(4)))
    corner = unmix(*(lane_sum(jnp.where(lane == i, edge_back_all[8], 0.0)) for i in range(4)))
    far_c, far_s = tab["far"][0, me], tab["far"][1, me]
    near = []
    for c, s in ((side_y[0], side_y[2]), (side_y[1], side_y[3])):
        near.append(jnp.concatenate([far_c * c + far_s * s, far_c * s - far_s * c], 1))
    near = jnp.concatenate(near + [jnp.zeros((SUB - 2, 2 * h), F32)], 0)
    last = product(split(near), both("wave_x"), flip=True)
    edge_c, edge_s = edge_rows[0:1], edge_rows[1:2]
    last_c = last[0:1] + corner[0] * edge_c + corner[2] * edge_s
    last_s = last[1:2] + corner[1] * edge_c + corner[3] * edge_s
    spread[...] = column(last_c) * edge_c + column(last_s) * edge_s
    col_c, col_s = column(edge_c), column(edge_s)

    wait_all(6, back_rows.at[0], lambda p: back_in.at[:, pl.ds(p * SUB, SUB), :])
    part_c = back_in[0].T + col_c * side_x[0] + col_s * side_x[2]
    part_s = back_in[1].T + col_c * side_x[1] + col_s * side_x[3]
    pair = split(jnp.concatenate([part_c, part_s], 1))
    adds = jnp.concatenate([spread[...], spread[...]], 1)
    stores = []
    for b in range(blocks):
        where = slice(b * block, (b + 1) * block)
        out[:, where] = product(pair, (tab["wave_y"][0, :, where], tab["wave_y"][1, :, where])) + adds
        stores.append(pltpu.make_async_copy(out.at[:, where], grad_hbm.at[:, where], out_sem.at[b]))
        stores[-1].start()
    drain(0, rows_t.at[:, pl.ds(0, SUB), :], rows_in.at[me])
    drain(1, edge_out.at[0], edge_in.at[me])
    drain(2, chunk.at[me], chunk.at[me])
    drain(3, edge_all.at[me], edge_all.at[me])
    drain(4, grad_t.at[:, pl.ds(0, SUB), :], grad_in.at[me])
    drain(5, edge_back.at[0], edge_back_in.at[me])
    drain(6, back_rows.at[0], back_in.at[:, pl.ds(0, SUB), :])
    drain(7, edge_back_all.at[me], edge_back_all.at[me])
    for store in stores:
        store.wait()


def fused(devices, mask_field, target_print, source_points, source_groups, group_logits, pupil_radius):
    rows, n = mask_field.shape
    h = K // 2
    coarse = 2 * K
    sources = source_points.shape[0]
    consts = tables(n, rows, devices)
    smem = pl.BlockSpec(memory_space=pltpu.SMEM)
    anywhere = pl.BlockSpec(memory_space=pl.ANY)
    vmem = lambda *shape: pltpu.VMEM(shape, F32)
    scratch = [pltpu.VMEM(consts[k].shape, consts[k].dtype) for k in NAMES] + [
        vmem(rows, n), pltpu.VMEM((rows, n), jnp.int32),
        vmem(2, h, rows), vmem(devices, 1, LANES), vmem(devices, 2, SUB, rows), vmem(devices, 1, LANES),
        vmem(devices, 4, SUB, h), vmem(devices, 1, LANES), vmem(h + SUB, 2 * h), vmem(4, 2, h, h),
        vmem(4, 2, h, h), vmem(sources, 2 * rows, coarse), vmem(rows, coarse), vmem(rows, coarse),
        vmem(4, 2, h, h), vmem(4, h, h), vmem(devices, 1, LANES), vmem(devices, 4, SUB, h),
        vmem(devices, 1, LANES), vmem(devices, 1, LANES), vmem(devices, 2, SUB, rows), vmem(2, h, rows),
        vmem(rows, LANES), vmem(rows, n),
        pltpu.SemaphoreType.DMA((12,)), pltpu.SemaphoreType.DMA((n // (2 * LANES),)),
        pltpu.SemaphoreType.DMA((8, devices)), pltpu.SemaphoreType.DMA((8, devices)),
    ]
    return pl.pallas_call(
        functools.partial(kernel, devices, n),
        out_shape=(
            jax.ShapeDtypeStruct((1,), F32),
            jax.ShapeDtypeStruct((rows, n), F32),
            jax.ShapeDtypeStruct((NG,), F32),
        ),
        in_specs=[smem] * 4 + [anywhere] * (2 + len(NAMES)),
        out_specs=(smem, anywhere, smem),
        scratch_shapes=scratch,
        compiler_params=pltpu.CompilerParams(
            collective_id=0, has_side_effects=True, vmem_limit_bytes=60 * 1024 * 1024
        ),
    )(source_points, source_groups, group_logits, pupil_radius, mask_field, target_print,
      *(jnp.asarray(consts[k]) for k in NAMES))


HIGH = lax.Precision.HIGH


def dot(form, left, right):
    return jnp.einsum(form, left, right, precision=HIGH, preferred_element_type=F32)


def waves(left, right, length):
    turns = angles(left, right, length)
    return np.cos(turns), np.sin(turns)


def shifted_waves(count, freq, length, device, devices):
    near = np.stack(waves(np.arange(count), freq, length)).astype(np.float32)
    far = np.stack(waves(np.arange(devices) * count, freq, length)).astype(np.float32)
    far = lax.dynamic_slice_in_dim(jnp.asarray(far), device, 1, axis=1)
    return far[0] * near[0] - far[1] * near[1], far[1] * near[0] + far[0] * near[1]


def exchange(blocks):
    return lax.all_to_all(blocks, "slab", 0, 0)


def plain(devices, mask_field, target_print, source_points, source_groups, group_logits, pupil_radius):
    rows, n = mask_field.shape
    sources = source_points.shape[0]
    coarse = 2 * K
    step = n // coarse
    cols = coarse // devices
    half = n // 2
    device = lax.axis_index("slab")
    freq = np.arange(K, dtype=np.int64) - K // 2
    order = np.concatenate([freq[freq % 2 == 0], freq[freq % 2 == 1]])
    kh = K // 2
    norming = 1.0 / (n * n)

    cos_y, sin_y = waves(np.arange(half), order, n)
    fold = [
        jnp.asarray(np.concatenate([t[:, p * kh : (p + 1) * kh] for t in (cos_y, sin_y)], 1), F32)
        for p in (0, 1)
    ]
    lag = np.mod(np.arange(n)[None, :] - step * np.arange(coarse)[:, None], n)
    response = np.zeros(n)
    for f in range(1, K):
        response += 2.0 * np.cos(2.0 * math.pi * np.mod(f * np.arange(n), n) / n)
    response = (response + 1.0) / coarse
    up = jnp.asarray(response[lag], F32)
    cos_c, sin_c = waves(freq, np.arange(coarse), coarse)
    wave_x = jnp.asarray(np.concatenate([cos_c, sin_c], 1), F32)
    loc_c, loc_s = shifted_waves(rows, freq, n, device, devices)
    loc = jnp.concatenate([loc_c, loc_s], 1)
    a, b = shifted_waves(cols, order, coarse, device, devices)
    lift = jnp.concatenate([jnp.concatenate([a, -b], 1), jnp.concatenate([b, a], 1)], 0)

    cutoff = pupil_radius[0]
    shifted = (source_points - GRID // 2) * cutoff // shift_scale
    first = jnp.asarray(freq, jnp.int32)[None, None, :] + shifted[:, 0, None, None]
    second = jnp.asarray(np.tile(order, 2), jnp.int32)[None, :, None] + shifted[:, 1, None, None]
    passed = first * first + second * second <= cutoff * cutoff

    near, away = mask_field[:, :half], mask_field[:, half:]
    even = dot("xy,yq->xq", near + away, fold[0])
    odd = dot("xy,yq->xq", near - away, fold[1])
    part_c = jnp.concatenate([even[:, :kh], odd[:, :kh]], 1)
    part_s = jnp.concatenate([even[:, kh:], odd[:, kh:]], 1)
    spec = dot("xq,xk->qk", jnp.concatenate([part_c, part_s], 1), loc)
    band = jnp.concatenate([spec[:K, :K] - spec[K:, K:], -(spec[:K, K:] + spec[K:, :K])], 0)
    band = jnp.sum(exchange(band.reshape(devices, 2 * K // devices, K)), 0)
    band = lax.all_gather(band, "slab", tiled=True)

    kept = jnp.where(passed, band[None], 0.0)
    wide = dot("aq,sqk->sak", lift, kept)
    both = dot("ak,kx->ax", wide.reshape(sources * 2 * cols, K), wave_x)
    both = both.reshape(sources, 2, cols, 2 * coarse)
    field_re = (both[:, 0, :, :coarse] - both[:, 1, :, coarse:]) * norming
    field_im = (both[:, 0, :, coarse:] + both[:, 1, :, :coarse]) * norming
    bright = field_re * field_re + field_im * field_im
    onehot = (source_groups[:, None] == jnp.arange(NG, dtype=jnp.int32)[None, :]).astype(F32)
    weights = jnp.exp(jnp.sum(onehot * group_logits[None, :], 1))
    share = weights / jnp.sum(weights)
    image = jnp.sum(share[:, None, None] * bright, 0)

    tall = dot("cm,mx->cx", image, up)
    tall = lax.all_to_all(tall, "slab", 1, 0, tiled=True)
    intensity = dot("cx,cy->xy", tall, up)
    resist = jax.nn.sigmoid(steepness * (intensity - threshold))
    misfit = resist - target_print.astype(F32)
    slope = (2.0 * steepness) * misfit * resist * (1.0 - resist)
    squares = jnp.sum(misfit * misfit)
    down = dot("xy,cy->cx", slope, up)
    down = lax.all_to_all(down, "slab", 0, 1, tiled=True)
    pull = dot("cx,mx->cm", down, up)

    per_source = jnp.sum(bright * pull[None], (1, 2))
    sums = jnp.concatenate([per_source, squares[None]])
    factor = (2.0 * norming) * share[:, None, None] * pull[None]
    back = jnp.stack([factor * field_re, factor * field_im], 1)
    low = dot("ax,kx->ak", back.reshape(sources * 2 * cols, coarse), wave_x[:, :coarse])
    lows = dot("ax,kx->ak", back.reshape(sources * 2 * cols, coarse), wave_x[:, coarse:])
    low = low.reshape(sources, 2, cols, K)
    lows = lows.reshape(sources, 2, cols, K)
    settle = jnp.concatenate([low[:, 0] + lows[:, 1], low[:, 1] - lows[:, 0]], 1)
    settle = dot("aq,sak->sqk", lift, settle)
    grad_band = jnp.sum(jnp.where(passed, settle, 0.0), 0).reshape(devices, 2 * K // devices, K)
    extra = jnp.pad(sums[None, :], ((0, 7), (0, K - sources - 1)))
    extra = jnp.broadcast_to(extra[None], (devices, 8, K))
    grad_band = jnp.sum(exchange(jnp.concatenate([grad_band, extra], 1)), 0)
    sums = grad_band[-8, : sources + 1]
    grad_band = lax.all_gather(grad_band[:-8], "slab", tiled=True)
    per_source, squares = sums[:-1], sums[-1]
    loss_value = (squares * norming).reshape(1)
    against = jnp.sum(share * per_source)
    source_pull = share * (per_source - against)
    group_grad = jnp.sum(onehot * source_pull[:, None], 0) * norming

    spread = dot("tk,qk->tq", jnp.concatenate([loc_c, loc_s], 0), grad_band)
    spread_re = spread[:rows, :K] - spread[rows:, K:]
    spread_im = spread[:rows, K:] + spread[rows:, :K]
    even = dot("xq,yq->xy", jnp.concatenate([spread_re[:, :kh], -spread_im[:, :kh]], 1), fold[0])
    odd = dot("xq,yq->xy", jnp.concatenate([spread_re[:, kh:], -spread_im[:, kh:]], 1), fold[1])
    mask_grad = jnp.concatenate([even + odd, even - odd], 1)
    return loss_value, mask_grad, group_grad


def on_device(devices, mask_field, *others):
    tiles = mask_field.shape[0] == LANES and K // 2 == LANES == SUB * devices and devices >= 10
    return (fused if tiles else plain)(devices, mask_field, *others)


def solution(mesh):
    in_specs = (
        P(("clip", "slab"), None),
        P(("clip", "slab"), None),
        P("clip", None),
        P("clip"),
        P("clip"),
        P("clip"),
    )
    out_specs = (P("clip"), P(("clip", "slab"), None), P("clip"))
    return jax.shard_map(
        functools.partial(on_device, mesh.shape["slab"]),
        mesh=mesh, in_specs=in_specs, out_specs=out_specs, check_vma=False,
    )
```

time: 151 us -> 82.2 us (0.54)
  blocking collectives: 88.5 us -> 0 us
  Pallas kernels: 0 us -> 74.7 us
  matrix products: 27.8 us -> 0 us
  waiting for transfers between devices: 12 us -> 0 us
  other arithmetic: 8.98 us -> 0 us
  starting transfers between devices: 7.41 us -> 0 us
  local copies, waits for them, and re-layouts: 2.46 us -> 4.17 us
    pallas_call x0 -> x1, Pallas kernels: none -> 74.7 us  [fused(): pl.pallas_call(functools.partial(kernel, devices, n), out_shape=(jax.Shap...]
    all_to_all x3 -> x0, blocking collectives: 46.7 us -> none  [the longest x1 21.1 us: exchange(): return lax.all_to_all(blocks, 'slab', 0, 0)]
    all_gather x2 -> x0, blocking collectives: 41.7 us -> none  [gather(): return lax.all_gather(block, 'slab', tiled=True)]
    dot_general x17 -> x0, matrix products: 27.8 us -> none  [dot(): jnp.einsum(form, left, right, precision=HIGH, preferred_element_type=jnp....]
    all_to_all x1 -> x0, waiting for transfers between devices: 12 us -> none  [exchange(): return lax.all_to_all(blocks, 'slab', 0, 0)]
    all_to_all x1 -> x0, starting transfers between devices: 7.41 us -> none  [exchange(): return lax.all_to_all(blocks, 'slab', 0, 0)]
    unnamed x36 -> x5, local copies, waits for them, and re-layouts: 0.52 us -> 4.17 us
    mul x6 -> x0, other arithmetic: 2.59 us -> none  [the longest x1 0.65 us: on_device(): factor = 2.0 * norming * share[:, None, None] * pull[None]]
  transfers between devices with their start and end apart: 1 -> 0, of which waited for: 1 -> 0; matrix products, arithmetic and copies ran while one was open for 1% -> 0% of each run, Pallas kernels for 0% -> 0%
where the time goes in v1:
time: 82.2 us; the launch traced here: 81.9 us
  Pallas kernels  74.7 us (91%)
  local copies, waits for them, and re-layouts  4.17 us (5%)
  between operations  3.06 us (4%)
    pallas_call x1, Pallas kernels, fused(): pl.pallas_call(functools.partial(kernel, devices, n), out_shape=(jax.Shap...  74.7 us
    unnamed x5, local copies, waits for them, and re-layouts  4.17 us

profile of v1, /device:TPU:0, one launch (start us, length us, event | category | flops | bytes accessed | tf_op | source)
XLA Modules:
  0.0 81.9 jit_solution(3816795097903443903)
XLA Ops:
  1.3 1.4 %copy.19.refs_0_ = s32[16,2]{1,0:T(8,128)} copy(s32[16,2]{0,1:T(2,128)} %param.18) | data formatting | bytes 256 | tf_op args[2]
  2.6 74.7 %shard_map.175 = (f32[1]{0:T(128)}, f32[128,2048]{1,0:T(8,128)}, f32[8]{0:T(128)}) custom-call(s32[16,2]{1,0:T(8,128)} %copy.19.refs_0_, s32[16]{0:T(128)} %refs_1_.1, f32[8]{0:T(128)} %refs_2_.1, s32[1]{0:T(128)S(6)} %copy.23.refs_3_, f32[128,2048]{1,0:T(8,128)} %refs_4_.1, s32[128,2048]{1,0:T(8,128)} %refs_5_.1, ...), custom_call_target="tpu_custom_call" | custom-call | tf_op jit(solution)/shard_map/pallas_call | solution.py:486
  77.4 0.0 copy-start
  78.0 2.3 %copy.25 = f32[128,2048]{1,0:T(8,128)} copy(f32[128,2048]{1,0:T(8,128)} %get-tuple-element.7) | data formatting | bytes 2097152
  80.3 0.0 copy-done
  80.3 0.5 copy.26
Async XLA Ops:
  77.4 2.9 %copy-start = (f32[8]{0:T(128)S(1)}, f32[8]{0:T(128)}, u32[]{:S(2)}) copy-start(f32[8]{0:T(128)} %get-tuple-element.8) | copy-start | bytes 100

commit v2 on v1

--- a/solution.py
+++ b/solution.py
@@ -78,7 +78,7 @@
         "wave_y": halves(wave_y),
         "wave_x": halves(wave_x),
         "half_x": halves(half_x),
-        "half_xt": halves(half_x.T),
+        "half_xt": np.concatenate(list(halves(half_x.T)[[0, 0, 1]]), 1),
         "half_y": halves(half_y),
         "half_yt": halves(half_y.T),
         "up": halves(up),
@@ -92,19 +92,20 @@
 
 
 def kernel(devices, n, *refs):
-    points, groups, logits, radius, mask_hbm, target_hbm = refs[:6]
+    small_hbm, mask_hbm, target_hbm = refs[:4], refs[4], refs[5]
     sources_in = dict(zip(NAMES, refs[6 : 6 + len(NAMES)]))
     refs = refs[6 + len(NAMES) :]
-    loss_ref, grad_hbm, group_ref = refs[:3]
-    refs = refs[3:]
+    result = refs[0]
+    refs = refs[1:]
     tab = dict(zip(NAMES, refs[: len(NAMES)]))
     refs = refs[len(NAMES) :]
     (mask, target, rows_t, edge_out, rows_in, edge_in, chunk, edge_all, ext, band, data, fields, image, pull,
-     grads, grad_t, edge_back, grad_in, edge_back_in, edge_back_all, back_rows, back_in, spread, out,
-     local_sem, out_sem, send_sem, recv_sem) = refs
+     grads, grad_t, edge_back, grad_in, edge_back_in, edge_back_all, back_rows, back_in,
+     folded, wides, weighed, settled, totals, points, groups, logits, radius,
+     local_sem, send_sem, recv_sem) = refs
     h = K // 2
     coarse = 2 * K
-    sources = points.shape[0]
+    sources = points.shape[1]
     rows = mask.shape[0]
     block = 2 * LANES
     blocks = n // block
@@ -113,8 +114,10 @@
     norming = 1.0 / (n * n)
 
     loads = {}
+    small = (points, groups, logits, radius)
     for i, (name, src, dst) in enumerate(
-        [("mask", mask_hbm, mask), ("wave_y", sources_in["wave_y"], tab["wave_y"])]
+        [(f"small{k}", small_hbm[k], small[k]) for k in range(4)]
+        + [("mask", mask_hbm, mask), ("wave_y", sources_in["wave_y"], tab["wave_y"])]
         + [(k, sources_in[k], tab[k]) for k in ("edge", "wave_x", "far", "half_far", "half_x", "half_y")]
         + [("up", sources_in["up"], tab["up"]), ("target", target_hbm, target)]
         + [(k, sources_in[k], tab[k]) for k in ("half_yt", "half_xt")]
@@ -170,15 +173,6 @@
 
     def column(row):
         return jnp.broadcast_to(row, (LANES, LANES)).T
-
-    logit_row = jnp.full((1, LANES), 0.0, F32)
-    group_row = jnp.full((1, LANES), -1, jnp.int32)
-    for s in range(sources):
-        g = groups[s]
-        logit_row = jnp.where(lane == s, logits[g], logit_row)
-        group_row = jnp.where(lane == s, g, group_row)
-    weight_row = jnp.where(lane < sources, jnp.exp(logit_row), 0.0)
-    share_row = weight_row / jnp.sum(weight_row, axis=1, keepdims=True)
 
     loads["mask"].wait()
     loads["wave_y"].wait()
@@ -227,6 +221,17 @@
     send_all(1, lambda p: edge_out.at[p], edge_in.at[me])
     rows_in[me] = rows_t[:, pl.ds(me * SUB, SUB), :]
     edge_in[me] = edge_out[me]
+
+    for k in range(4):
+        loads[f"small{k}"].wait()
+    logit_row = jnp.full((1, LANES), 0.0, F32)
+    group_row = jnp.full((1, LANES), -1, jnp.int32)
+    for s in range(sources):
+        g = groups[s]
+        logit_row = jnp.where(lane == s, logits[g], logit_row)
+        group_row = jnp.where(lane == s, g, group_row)
+    weight_row = jnp.where(lane < sources, jnp.exp(logit_row), 0.0)
+    share_row = weight_row / jnp.sum(weight_row, axis=1, keepdims=True)
 
     wait_all(0, rows_t.at[:, pl.ds(0, SUB), :], lambda p: rows_in.at[p])
     gathered = rows_in[...].reshape(devices * 2 * SUB, rows)
@@ -282,42 +287,78 @@
 
     cutoff = radius[0]
     limit = (cutoff * cutoff).astype(F32)
-    row_index = lax.broadcasted_iota(jnp.int32, (h, h), 0).astype(F32)
     lane_index = lane.astype(F32)
+    chunk_rows = [slice(c, c + 2 * SUB) for c in range(0, h, 2 * SUB)]
+    row_index = lax.broadcasted_iota(jnp.int32, (2 * SUB, LANES), 0).astype(F32)
 
     def masks(s):
-        first = ((points[s, 0] - GRID // 2) * cutoff // shift_scale).astype(F32)
-        second = ((points[s, 1] - GRID // 2) * cutoff // shift_scale).astype(F32)
-        row_p, row_m = row_index + first, first - 1.0 - row_index
+        first = ((points[0, s] - GRID // 2) * cutoff // shift_scale).astype(F32)
+        second = ((points[1, s] - GRID // 2) * cutoff // shift_scale).astype(F32)
         col_p, col_m = lane_index + second, second - 1.0 - lane_index
-        room_p, room_m = limit - row_p * row_p, limit - row_m * row_m
         col_p, col_m = col_p * col_p, col_m * col_m
-        return col_p <= room_p, col_m <= room_p, col_p <= room_m, col_m <= room_m
+
+        def of(where):
+            row_p = row_index + (first + where.start)
+            row_m = (first - 1.0 - where.start) - row_index
+            room_p, room_m = limit - row_p * row_p, limit - row_m * row_m
+            return col_p <= room_p, col_m <= room_p, col_p <= room_m, col_m <= room_m
+
+        return of
 
     def share_of(s):
         return lane_sum(jnp.where(lane == s, share_row, 0.0))
 
+    def keep(ref, where, lanes, value):
+        high, low = split(value)
+        ref[0, where, lanes] = high
+        ref[1, where, lanes] = low
+
+    unroll = 8
+    quarter = [slice(i * h, (i + 1) * h) for i in range(4)]
     image[...] = jnp.zeros_like(image)
 
-    def forward(s, carry):
+    def mask_band(s, slot):
         kept = masks(s)
-        quads = []
-        for part in range(2):
-            pp, pm, mp, mm = (jnp.where(kept[q], band[q, part], 0.0) for q in range(4))
-            ep, op, em, om = pp + mp, pp - mp, pm + mm, pm - mm
-            quads.append((ep + em, ep - em, op + om, op - om))
-        (ee_r, eo_r, oe_r, oo_r), (ee_i, eo_i, oe_i, oo_i) = quads
-        top = jnp.concatenate([ee_r, -eo_i, ee_i, eo_r], 1)
-        low = jnp.concatenate([oe_i, oo_r, -oe_r, oo_i], 1)
-        wide = product(both("half_x"), split(jnp.concatenate([top, low], 0)))
-        wide = jnp.concatenate([wide[:, : 2 * h], wide[:, 2 * h :]], 0)
-        field = product(split(wide), both("half_y"))
+        dest = folded.at[slot]
+        for where in chunk_rows:
+            keeps = kept(where)
+            low_where = slice(where.start + h, where.stop + h)
+            pp, pm, mp, mm = (jnp.where(keeps[q], band[q, 0, where, :], 0.0) for q in range(4))
+            ep, em, op, om = pp + mp, pm + mm, mp - pp, mm - pm
+            keep(dest, where, quarter[0], ep + em)
+            keep(dest, where, quarter[3], ep - em)
+            keep(dest, low_where, quarter[1], om - op)
+            keep(dest, low_where, quarter[2], op + om)
+            pp, pm, mp, mm = (jnp.where(keeps[q], band[q, 1, where, :], 0.0) for q in range(4))
+            ep, em, op, om = pp + mp, pm + mm, pp - mp, pm - mm
+            keep(dest, where, quarter[1], em - ep)
+            keep(dest, where, quarter[2], ep + em)
+            keep(dest, low_where, quarter[0], op + om)
+            keep(dest, low_where, quarter[3], op - om)
+
+    def to_rows(slot):
+        wide = product(both("half_x"), (folded[slot, 0], folded[slot, 1]))
+        keep(wides.at[slot], slice(0, rows), slice(None), wide[:, : 2 * h])
+        keep(wides.at[slot], slice(rows, 2 * rows), slice(None), wide[:, 2 * h :])
+
+    def to_field(s, slot):
+        field = product((wides[slot, 0], wides[slot, 1]), both("half_y"))
         fields[s] = field
         re, im = field[:rows], field[rows:]
         image[...] += share_of(s) * (re * re + im * im)
+
+    def forward(i, carry):
+        base = i * unroll
+        for t in range(unroll + 2):
+            if t < unroll:
+                mask_band(base + t, t)
+            if 0 <= t - 1 < unroll:
+                to_rows(t - 1)
+            if 0 <= t - 2 < unroll:
+                to_field(base + t - 2, t - 2)
         return carry
 
-    lax.fori_loop(0, sources, forward, 0)
+    lax.fori_loop(0, sources // unroll, forward, 0)
 
     loads["up"].wait()
     loads["target"].wait()
@@ -340,28 +381,63 @@
     loads["half_yt"].wait()
     loads["half_xt"].wait()
     grads[...] = jnp.zeros_like(grads)
-
-    def backward(s, sums):
+    half_xt = tab["half_xt"]
+
+    def weigh(s, slot):
+        dest = weighed.at[slot]
+        total = jnp.zeros((2 * SUB, coarse), F32)
+        for start in range(0, rows, 2 * SUB):
+            where = slice(start, start + 2 * SUB)
+            other = slice(start + rows, start + rows + 2 * SUB)
+            weak, re, im = pull[where, :], fields[s, where, :], fields[s, other, :]
+            down_r, down_i = weak * re, weak * im
+            total = total + (down_r * re + down_i * im)
+            keep(dest, where, slice(None), down_r)
+            keep(dest, other, slice(None), down_i)
+        total = total[:SUB] + total[SUB:]
+        totals[s] = total[:, :h] + total[:, h : 2 * h] + total[:, 2 * h : 3 * h] + total[:, 3 * h :]
+
+    def from_field(s, slot):
+        settle = product((weighed[slot, 0], weighed[slot, 1]), both("half_yt")) * (2.0 * share_of(s))
+        for part in range(2):
+            high, low = split(settle[part * rows : (part + 1) * rows])
+            settled[slot, :rows, part * 2 * h : (part + 1) * 2 * h] = high
+            settled[slot, rows:, part * 2 * h : (part + 1) * 2 * h] = low
+
+    def from_rows(s, slot):
         kept = masks(s)
-        re, im = fields[s, :rows], fields[s, rows:]
-        weak = pull[...]
-        down_r, down_i = weak * re, weak * im
-        total = lane_sum(jnp.sum(down_r * re + down_i * im, 0, keepdims=True))
-        sums = jnp.where(lane == s, total, sums)
-        scale = 2.0 * share_of(s)
-        back = jnp.concatenate([down_r, down_i], 0)
-        settle = product(split(back), both("half_yt")) * scale
-        settle = jnp.concatenate([settle[:rows], settle[rows:]], 1)
-        full = product(both("half_xt"), split(settle))
-        ee_r, eo_i, ee_i, eo_r = full[:h, :h], -full[:h, h : 2 * h], full[:h, 2 * h : 3 * h], full[:h, 3 * h :]
-        oe_i, oo_r, oe_r, oo_i = full[h:, :h], full[h:, h : 2 * h], -full[h:, 2 * h : 3 * h], full[h:, 3 * h :]
-        for part, (ee, eo, oe, oo) in enumerate(((ee_r, eo_r, oe_r, oo_r), (ee_i, eo_i, oe_i, oo_i))):
-            ep, em, op, om = ee + eo, ee - eo, oe + oo, oe - oo
+        dims = (((1,), (0,)), ((), ()))
+        full = lax.dot_general(half_xt[:, : 2 * rows], settled[slot], dims, preferred_element_type=F32)
+        full = full + lax.dot_general(
+            half_xt[:, 2 * rows :], settled[slot, :rows], dims, preferred_element_type=F32
+        )
+        for where in chunk_rows:
+            keeps = kept(where)
+            top, low = full[where], full[where.start + h : where.stop + h]
+            ee_r, no_i, ee_i, eo_r = (top[:, q] for q in quarter)
+            oe_i, oo_r, ne_r, oo_i = (low[:, q] for q in quarter)
+            ep, em, op, om = ee_r + eo_r, ee_r - eo_r, oo_r - ne_r, -ne_r - oo_r
             for q, value in enumerate((ep + op, em + om, ep - op, em - om)):
-                grads[q, part] += jnp.where(kept[q], value, 0.0)
-        return sums
-
-    sums = lax.fori_loop(0, sources, backward, jnp.zeros((1, LANES), F32))
+                grads[q, 0, where, :] += jnp.where(keeps[q], value, 0.0)
+            ep, em, op, om = ee_i - no_i, ee_i + no_i, oe_i + oo_i, oe_i - oo_i
+            for q, value in enumerate((ep + op, em + om, ep - op, em - om)):
+                grads[q, 1, where, :] += jnp.where(keeps[q], value, 0.0)
+
+    def backward(i, carry):
+        base = i * unroll
+        for t in range(unroll + 2):
+            if t < unroll:
+                weigh(base + t, t)
+            if 0 <= t - 1 < unroll:
+                from_field(base + t - 1, t - 1)
+            if 0 <= t - 2 < unroll:
+                from_rows(base + t - 2, t - 2)
+        return carry
+
+    lax.fori_loop(0, sources // unroll, backward, 0)
+    each = lane_sum(jnp.sum(totals[...], 1))
+    own = lax.broadcasted_iota(jnp.int32, (sources, LANES), 0) == lane
+    sums = jnp.sum(jnp.where(own, each, 0.0), 0, keepdims=True)
     sums = jnp.where(lane == sources, squares, sums)
 
     def unturn(slot, sign):
@@ -419,11 +495,11 @@
     wait_all(7, edge_back_all.at[me], lambda p: edge_back_all.at[p])
 
     sums = edge_back_all[9]
-    loss_ref[0] = jnp.sum(jnp.where(lane == sources, sums, 0.0)) * norming
+    small_at = slice(2 * h + LANES, 2 * h + 2 * LANES)
+    result[0:1, small_at] = sums * norming
     sums = jnp.where(lane < sources, sums, 0.0)
-    source_pull = share_row * (sums - lane_sum(share_row * sums))
-    for g in range(NG):
-        group_ref[g] = jnp.sum(jnp.where(group_row == g, source_pull, 0.0)) * norming
+    result[1:2, small_at] = share_row * (sums - lane_sum(share_row * sums)) * norming
+    result[2:3, small_at] = group_row.astype(F32)
 
     side_x = unmix(*(edge_back_all[i] for i in range(4)))
     side_y = unmix(*(edge_back_all[4 + i] for i in range(4)))
@@ -437,20 +513,14 @@
     edge_c, edge_s = edge_rows[0:1], edge_rows[1:2]
     last_c = last[0:1] + corner[0] * edge_c + corner[2] * edge_s
     last_s = last[1:2] + corner[1] * edge_c + corner[3] * edge_s
-    spread[...] = column(last_c) * edge_c + column(last_s) * edge_s
+    result[:, 2 * h : 2 * h + LANES] = column(last_c) * edge_c + column(last_s) * edge_s
     col_c, col_s = column(edge_c), column(edge_s)
 
     wait_all(6, back_rows.at[0], lambda p: back_in.at[:, pl.ds(p * SUB, SUB), :])
     part_c = back_in[0].T + col_c * side_x[0] + col_s * side_x[2]
     part_s = back_in[1].T + col_c * side_x[1] + col_s * side_x[3]
-    pair = split(jnp.concatenate([part_c, part_s], 1))
-    adds = jnp.concatenate([spread[...], spread[...]], 1)
-    stores = []
-    for b in range(blocks):
-        where = slice(b * block, (b + 1) * block)
-        out[:, where] = product(pair, (tab["wave_y"][0, :, where], tab["wave_y"][1, :, where])) + adds
-        stores.append(pltpu.make_async_copy(out.at[:, where], grad_hbm.at[:, where], out_sem.at[b]))
-        stores[-1].start()
+    result[:, :h] = part_c
+    result[:, h : 2 * h] = part_s
     drain(0, rows_t.at[:, pl.ds(0, SUB), :], rows_in.at[me])
     drain(1, edge_out.at[0], edge_in.at[me])
     drain(2, chunk.at[me], chunk.at[me])
@@ -459,6 +529,31 @@
     drain(5, edge_back.at[0], edge_back_in.at[me])
     drain(6, back_rows.at[0], back_in.at[:, pl.ds(0, SUB), :])
     drain(7, edge_back_all.at[me], edge_back_all.at[me])
+
+
+def closing(n, sources, result, wave, loss_hbm, grad_hbm, group_hbm, loss, group, out, out_sem):
+    block = 2 * LANES
+    blocks = n // block
+    lane = lax.broadcasted_iota(jnp.int32, (1, LANES), 1)
+    h = K // 2
+    small = result.at[:, 2 * h + LANES :]
+    loss[0] = jnp.sum(jnp.where(lane == sources, small[0:1, :], 0.0))
+    for g in range(NG):
+        group[g] = jnp.sum(jnp.where(small[2:3, :] == g, small[1:2, :], 0.0))
+    stores = [
+        pltpu.make_async_copy(loss, loss_hbm, out_sem.at[blocks]),
+        pltpu.make_async_copy(group, group_hbm, out_sem.at[blocks + 1]),
+    ]
+    for store in stores:
+        store.start()
+    pair = split(result[:, : 2 * h])
+    spread = result[:, 2 * h : 2 * h + LANES]
+    adds = jnp.concatenate([spread, spread], 1)
+    for b in range(blocks):
+        where = slice(b * block, (b + 1) * block)
+        out[:, where] = product(pair, (wave[0, :, where], wave[1, :, where])) + adds
+        stores.append(pltpu.make_async_copy(out.at[:, where], grad_hbm.at[:, where], out_sem.at[b]))
+        stores[-1].start()
     for store in stores:
         store.wait()
 
@@ -469,8 +564,7 @@
     coarse = 2 * K
     sources = source_points.shape[0]
     consts = tables(n, rows, devices)
-    smem = pl.BlockSpec(memory_space=pltpu.SMEM)
-    anywhere = pl.BlockSpec(memory_space=pl.ANY)
+    anywhere = pl.BlockSpec(memory_space=pltpu.HBM)
     vmem = lambda *shape: pltpu.VMEM(shape, F32)
     scratch = [pltpu.VMEM(consts[k].shape, consts[k].dtype) for k in NAMES] + [
         vmem(rows, n), pltpu.VMEM((rows, n), jnp.int32),
@@ -479,25 +573,43 @@
         vmem(4, 2, h, h), vmem(sources, 2 * rows, coarse), vmem(rows, coarse), vmem(rows, coarse),
         vmem(4, 2, h, h), vmem(4, h, h), vmem(devices, 1, LANES), vmem(devices, 4, SUB, h),
         vmem(devices, 1, LANES), vmem(devices, 1, LANES), vmem(devices, 2, SUB, rows), vmem(2, h, rows),
-        vmem(rows, LANES), vmem(rows, n),
-        pltpu.SemaphoreType.DMA((12,)), pltpu.SemaphoreType.DMA((n // (2 * LANES),)),
+        pltpu.VMEM((8, 2, 2 * h, coarse), BF16), pltpu.VMEM((8, 2, 2 * rows, 2 * h), BF16),
+        pltpu.VMEM((8, 2, 2 * rows, coarse), BF16), pltpu.VMEM((8, 2 * rows, coarse), BF16),
+        vmem(sources, SUB, LANES),
+        pltpu.SMEM((2, sources), jnp.int32), pltpu.SMEM((sources,), jnp.int32), pltpu.SMEM((NG,), F32),
+        pltpu.SMEM((1,), jnp.int32),
+        pltpu.SemaphoreType.DMA((16,)),
         pltpu.SemaphoreType.DMA((8, devices)), pltpu.SemaphoreType.DMA((8, devices)),
     ]
+    arrays = [jnp.asarray(consts[k]) for k in NAMES]
+    inside = pl.BlockSpec(memory_space=pltpu.VMEM)
+    (result,) = pl.pallas_call(
+        functools.partial(kernel, devices, n),
+        out_shape=(
+            jax.ShapeDtypeStruct((rows, 2 * h + 2 * LANES), F32),
+        ),
+        in_specs=[anywhere] * (6 + len(NAMES)),
+        out_specs=(inside,),
+        scratch_shapes=scratch,
+        compiler_params=pltpu.CompilerParams(
+            collective_id=0, has_side_effects=True, vmem_limit_bytes=58 * 1024 * 1024
+        ),
+    )(source_points.T, source_groups, group_logits, pupil_radius, mask_field, target_print, *arrays)
     return pl.pallas_call(
-        functools.partial(kernel, devices, n),
+        functools.partial(closing, n, sources),
         out_shape=(
             jax.ShapeDtypeStruct((1,), F32),
             jax.ShapeDtypeStruct((rows, n), F32),
             jax.ShapeDtypeStruct((NG,), F32),
         ),
-        in_specs=[smem] * 4 + [anywhere] * (2 + len(NAMES)),
-        out_specs=(smem, anywhere, smem),
-        scratch_shapes=scratch,
-        compiler_params=pltpu.CompilerParams(
-            collective_id=0, has_side_effects=True, vmem_limit_bytes=60 * 1024 * 1024
-        ),
-    )(source_points, source_groups, group_logits, pupil_radius, mask_field, target_print,
-      *(jnp.asarray(consts[k]) for k in NAMES))
+        in_specs=[inside] * 2,
+        out_specs=(anywhere, anywhere, anywhere),
+        scratch_shapes=[
+            pltpu.SMEM((1,), F32), pltpu.SMEM((NG,), F32), vmem(rows, n),
+            pltpu.SemaphoreType.DMA((n // (2 * LANES) + 2,)),
+        ],
+        compiler_params=pltpu.CompilerParams(vmem_limit_bytes=8 * 1024 * 1024),
+    )(result, arrays[0])
 
 
 HIGH = lax.Precision.HIGH

time: 82.2 us -> 63.9 us (0.78)
  Pallas kernels: 74.7 us -> 61.5 us
  local copies, waits for them, and re-layouts: 4.17 us -> 0.95 us
  between operations: 3.06 us -> 1.31 us
    pallas_call x1, Pallas kernels: 74.7 us -> 60.1 us  [fused(): pl.pallas_call(functools.partial(kernel, devices, n), out_shape=(jax.Shap...]
    unnamed x5 -> x4, local copies, waits for them, and re-layouts: 4.17 us -> 0.95 us
    pallas_call x0 -> x1, Pallas kernels: none -> 1.39 us  [fused(): pl.pallas_call(functools.partial(closing, n, sources), out_shape=(jax.Sha...]
where the time goes in v2:
time: 63.9 us; the launch traced here: 63.8 us
  Pallas kernels  61.5 us (96%)
  between operations  1.31 us (2%)
  local copies, waits for them, and re-layouts  0.95 us (1%)
    pallas_call x1, Pallas kernels, fused(): pl.pallas_call(functools.partial(kernel, devices, n), out_shape=(jax.Shap...  60.1 us
    pallas_call x1, Pallas kernels, fused(): pl.pallas_call(functools.partial(closing, n, sources), out_shape=(jax.Sha...  1.39 us

profile of v2, /device:TPU:0, one launch (start us, length us, event | category | flops | bytes accessed | tf_op | source)
XLA Modules:
  0.0 63.8 jit_solution(14536696240890976692)
XLA Ops:
  1.3 0.0 copy-start
  1.3 60.1 %shard_map.175.result = f32[128,512]{1,0:T(8,128)} custom-call(s32[2,16]{1,0:T(2,128)} %bitcast.1, s32[16]{0:T(128)} %refs_1_.1, f32[8]{0:T(128)} %refs_2_.1, s32[1]{0:T(128)S(6)} %copy.19.refs_3_, f32[128,2048]{1,0:T(8,128)} %refs_4_.1, s32[128,2048]{1,0:T(8,128)} %refs_5_.1, bf16[2,256,2048]{2,1,0:T(8,128)(2,1)} %constant.20.clone.refs_6_.wave, ...), custom_call_target="tpu_custom_call" | custom-call | tf_op jit(solution)/shard_map/pallas_call | solution.py:586
  61.4 0.0 copy-done
  61.4 0.0 copy-start.1
  61.4 0.9 %copy-done.1 = f32[128,512]{1,0:T(8,128)S(1)} copy-done((f32[128,512]{1,0:T(8,128)S(1)}, f32[128,512]{1,0:T(8,128)}, u32[]{:S(2)}) %copy-start.1) | copy-done | bytes 262168
  62.4 1.4 %shard_map.176 = (f32[1]{0:T(128)}, f32[128,2048]{1,0:T(8,128)}, f32[8]{0:T(128)}) custom-call(f32[128,512]{1,0:T(8,128)S(1)} %copy-done.1, bf16[2,256,2048]{2,1,0:T(8,128)(2,1)S(1)} %copy-done), custom_call_target="tpu_custom_call" | custom-call | tf_op jit(solution)/shard_map/pallas_call | solution.py:598
Async XLA Ops:
  1.3 60.1 %copy-start = (bf16[2,256,2048]{2,1,0:T(8,128)(2,1)S(1)}, bf16[2,256,2048]{2,1,0:T(8,128)(2,1)}, u32[]{:S(2)}) copy-start(bf16[2,256,2048]{2,1,0:T(8,128)(2,1)} %constant.20.clone.refs_6_.wave) | copy-start | bytes 6291460
  61.4 1.0 %copy-start.1 = (f32[128,512]{1,0:T(8,128)S(1)}, f32[128,512]{1,0:T(8,128)}, u32[]{:S(2)}) copy-start(f32[128,512]{1,0:T(8,128)} %shard_map.175.result) | copy-start | bytes 786436

commit v3 on v2

--- a/solution.py
+++ b/solution.py
@@ -102,7 +102,7 @@
     (mask, target, rows_t, edge_out, rows_in, edge_in, chunk, edge_all, ext, band, data, fields, image, pull,
      grads, grad_t, edge_back, grad_in, edge_back_in, edge_back_all, back_rows, back_in,
      folded, wides, weighed, settled, totals, points, groups, logits, radius,
-     local_sem, send_sem, recv_sem) = refs
+     pair_in, pair_sum, up_t, slopes, local_sem, send_sem, recv_sem, near_sem) = refs
     h = K // 2
     coarse = 2 * K
     sources = points.shape[1]
@@ -112,12 +112,24 @@
     step = n // coarse
     me = lax.axis_index("slab")
     norming = 1.0 / (n * n)
+    chips = devices // 2
+    core, chip = lax.rem(me, 2), me // 2
+    partner = me + 1 - 2 * core
+    most = pl.ds(0, devices - 1)
 
     loads = {}
     small = (points, groups, logits, radius)
+    pieces = [slice(c, c + n // 4) for c in range(0, n, n // 4)]
     for i, (name, src, dst) in enumerate(
-        [(f"small{k}", small_hbm[k], small[k]) for k in range(4)]
-        + [("mask", mask_hbm, mask), ("wave_y", sources_in["wave_y"], tab["wave_y"])]
+        [
+            piece
+            for k, where in enumerate(pieces)
+            for piece in (
+                (f"mask{k}", mask_hbm.at[:, where], mask.at[:, where]),
+                (f"wave_y{k}", sources_in["wave_y"].at[:, :, where], tab["wave_y"].at[:, :, where]),
+            )
+        ]
+        + [(f"small{k}", small_hbm[k], small[k]) for k in range(4)]
         + [(k, sources_in[k], tab[k]) for k in ("edge", "wave_x", "far", "half_far", "half_x", "half_y")]
         + [("up", sources_in["up"], tab["up"]), ("target", target_hbm, target)]
         + [(k, sources_in[k], tab[k]) for k in ("half_yt", "half_xt")]
@@ -136,10 +148,10 @@
     def both(name):
         return tab[name][0], tab[name][1]
 
-    def copy_to(phase, peer, src, dst):
+    def copy_to(phase, peer, src, dst, sem=None):
         return pltpu.make_async_remote_copy(
-            src_ref=src, dst_ref=dst, send_sem=send_sem.at[phase, peer], recv_sem=recv_sem.at[phase, me],
-            device_id={"slab": peer},
+            src_ref=src, dst_ref=dst, send_sem=send_sem.at[phase],
+            recv_sem=recv_sem.at[phase] if sem is None else sem, device_id={"slab": peer},
         )
 
     def send_all(phase, src_of, dst):
@@ -150,33 +162,23 @@
 
         lax.fori_loop(1, devices, body, 0)
 
-    def wait_all(phase, src, dst_of):
-        def body(i, carry):
-            peer = lax.rem(me + i, devices)
-            pltpu.make_async_remote_copy(
-                src_ref=src, dst_ref=dst_of(peer), send_sem=send_sem.at[phase, peer],
-                recv_sem=recv_sem.at[phase, peer], device_id={"slab": peer},
-            ).wait_recv()
-            return carry
-
-        lax.fori_loop(1, devices, body, 0)
-
-    def drain(phase, src, dst):
-        def body(i, carry):
-            peer = lax.rem(me + i, devices)
-            copy_to(phase, peer, src, dst).wait_send()
-            return carry
-
-        lax.fori_loop(1, devices, body, 0)
+    def wait_all(phase, ref, sem=None):
+        copy_to(phase, partner, ref, ref, sem).wait_recv()
+
+    def drain(phase, ref):
+        copy_to(phase, partner, ref, ref).wait_send()
 
     lane = lax.broadcasted_iota(jnp.int32, (1, LANES), 1)
 
     def column(row):
         return jnp.broadcast_to(row, (LANES, LANES)).T
 
-    loads["mask"].wait()
-    loads["wave_y"].wait()
-    transformed = product(split(mask[...]), both("wave_y"), flip=True)
+    transformed = 0.0
+    for k, where in enumerate(pieces):
+        loads[f"mask{k}"].wait()
+        loads[f"wave_y{k}"].wait()
+        wave = (tab["wave_y"][0, :, where], tab["wave_y"][1, :, where])
+        transformed = transformed + product(split(mask[:, where]), wave, flip=True)
     rows_t[0] = transformed[:, :h].T
     rows_t[1] = transformed[:, h:].T
     loads["edge"].wait()
@@ -233,7 +235,14 @@
     weight_row = jnp.where(lane < sources, jnp.exp(logit_row), 0.0)
     share_row = weight_row / jnp.sum(weight_row, axis=1, keepdims=True)
 
-    wait_all(0, rows_t.at[:, pl.ds(0, SUB), :], lambda p: rows_in.at[p])
+    loads["up"].wait()
+    extra = (n - block) // step
+    for b in range(blocks):
+        start = extra - b * (block // step)
+        for part in range(2):
+            up_t[part, b * block : (b + 1) * block, :] = tab["up"][part, start : start + coarse, :].T
+
+    wait_all(0, rows_in.at[most])
     gathered = rows_in[...].reshape(devices * 2 * SUB, rows)
     turned = product(split(gathered), both("wave_x")).reshape(devices, 2 * SUB, 2 * h)
     far_c, far_s = tab["far"][0], tab["far"][1]
@@ -242,8 +251,14 @@
     sum_s = jnp.sum(far_s * turned_c + far_c * turned_s, 0)
     for i, value in enumerate(mixes(sum_c[:SUB], sum_c[SUB:], sum_s[:SUB], sum_s[SUB:])):
         chunk[me, i] = value
-    send_all(2, lambda p: chunk.at[me], chunk.at[me])
-    wait_all(1, edge_out.at[0], lambda p: edge_in.at[p])
+
+    def share(i, carry):
+        copy_to(2, lax.rem(me + 2 * i, devices), chunk.at[me], chunk.at[me], near_sem.at[chip]).start()
+        return carry
+
+    lax.fori_loop(1, chips, share, 0)
+    copy_to(2, partner, chunk.at[me], chunk.at[me]).start()
+    wait_all(1, edge_in.at[most])
     edge_all[me] = jnp.sum(edge_in[...], 0)
     send_all(3, lambda p: edge_all.at[me], edge_all.at[me])
 
@@ -253,8 +268,16 @@
     turn_c = column(tab["half_far"][0, me])
     turn_s = column(tab["half_far"][1, me])
 
-    wait_all(2, chunk.at[me], lambda p: chunk.at[p])
-    wait_all(3, edge_all.at[me], lambda p: edge_all.at[p])
+
+    def relay(i, carry):
+        peer = lax.rem(me + 2 * i, devices)
+        wait_all(2, chunk.at[peer], near_sem.at[peer // 2])
+        copy_to(2, partner, chunk.at[peer], chunk.at[peer]).start()
+        return carry
+
+    lax.fori_loop(1, chips, relay, 0)
+    wait_all(2, chunk.at[pl.ds(0, chips)])
+    wait_all(3, edge_all.at[most])
     shifted = []
     plain = []
     for i in range(4):
@@ -360,22 +383,21 @@
 
     lax.fori_loop(0, sources // unroll, forward, 0)
 
-    loads["up"].wait()
     loads["target"].wait()
-    pull[...] = jnp.zeros_like(pull)
     squares = jnp.zeros((rows, LANES), F32)
     image_pair = split(image[...])
-    extra = (n - block) // step
     for b in range(blocks):
         start = extra - b * (block // step)
+        where = slice(b * block, (b + 1) * block)
         up = (tab["up"][0, start : start + coarse, :], tab["up"][1, start : start + coarse, :])
         intensity = product(image_pair, up)
         resist = 1.0 / (1.0 + jnp.exp(-steepness * (intensity - threshold)))
-        misfit = resist - target[:, b * block : (b + 1) * block].astype(F32)
+        misfit = resist - target[:, where].astype(F32)
         slope = (2.0 * steepness) * misfit * resist * (1.0 - resist)
         square = misfit * misfit
         squares = squares + square[:, :LANES] + square[:, LANES:]
-        pull[...] += product(split(slope), up, flip=True)
+        keep(slopes, slice(0, rows), where, slope)
+    pull[...] = product((slopes[0], slopes[1]), (up_t[0], up_t[1]))
     squares = lane_sum(jnp.sum(squares, 0, keepdims=True))
 
     loads["half_yt"].wait()
@@ -460,7 +482,8 @@
             moved = pltpu.roll(ext[...], 1, 1)
             ext[...] = moved
             ext[1 : h + 1, :h] += second
-        grad_t[i] = ext[:h, :h].T
+        grad_t[i] = ext[:h, :h].T.reshape(chips, 2, SUB, h)
+        copy_to(8, partner, grad_t.at[i, :, 1 - core], pair_in.at[i]).start()
         edge_back[i] = ext[h : h + 1, :h]
         edge_back[4 + i] = ext[:h, h:].T[0:1, :]
         last_row = jnp.where(lane == i, ext[h : h + 1, h : h + 1], last_row)
@@ -469,11 +492,20 @@
     for i in range(10, devices):
         edge_back[i] = jnp.zeros((1, LANES), F32)
 
-    send_all(4, lambda p: grad_t.at[:, pl.ds(p * SUB, SUB), :], grad_in.at[me])
     send_all(5, lambda p: edge_back.at[p], edge_back_in.at[me])
-    grad_in[me] = grad_t[:, pl.ds(me * SUB, SUB), :]
     edge_back_in[me] = edge_back[me]
-    wait_all(4, grad_t.at[:, pl.ds(0, SUB), :], lambda p: grad_in.at[p])
+    wait_all(8, pair_in)
+    for i in range(4):
+        pair_sum[:, i] = grad_t[i, :, core] + pair_in[i]
+
+    def hand_over(i, carry):
+        peer = lax.rem(me + 2 * i, devices)
+        copy_to(4, peer, pair_sum.at[peer // 2], grad_in.at[chip]).start()
+        return carry
+
+    lax.fori_loop(1, chips, hand_over, 0)
+    grad_in[chip] = pair_sum[chip]
+    wait_all(4, grad_in.at[pl.ds(0, chips - 1)])
 
     def unmix(u, v, wp, wm):
         return u + v, wp - wm, wp + wm, v - u
@@ -489,10 +521,10 @@
     back_rows[...] = gathered.reshape(devices, 2, SUB, rows)
     send_all(6, lambda p: back_rows.at[p], back_in.at[:, pl.ds(me * SUB, SUB), :])
     back_in[:, pl.ds(me * SUB, SUB), :] = back_rows[me]
-    wait_all(5, edge_back.at[0], lambda p: edge_back_in.at[p])
+    wait_all(5, edge_back_in.at[most])
     edge_back_all[me] = jnp.sum(edge_back_in[...], 0)
     send_all(7, lambda p: edge_back_all.at[me], edge_back_all.at[me])
-    wait_all(7, edge_back_all.at[me], lambda p: edge_back_all.at[p])
+    wait_all(7, edge_back_all.at[most])
 
     sums = edge_back_all[9]
     small_at = slice(2 * h + LANES, 2 * h + 2 * LANES)
@@ -516,19 +548,20 @@
     result[:, 2 * h : 2 * h + LANES] = column(last_c) * edge_c + column(last_s) * edge_s
     col_c, col_s = column(edge_c), column(edge_s)
 
-    wait_all(6, back_rows.at[0], lambda p: back_in.at[:, pl.ds(p * SUB, SUB), :])
+    wait_all(6, back_in.at[:, pl.ds(0, h - SUB), :])
     part_c = back_in[0].T + col_c * side_x[0] + col_s * side_x[2]
     part_s = back_in[1].T + col_c * side_x[1] + col_s * side_x[3]
     result[:, :h] = part_c
     result[:, h : 2 * h] = part_s
-    drain(0, rows_t.at[:, pl.ds(0, SUB), :], rows_in.at[me])
-    drain(1, edge_out.at[0], edge_in.at[me])
-    drain(2, chunk.at[me], chunk.at[me])
-    drain(3, edge_all.at[me], edge_all.at[me])
-    drain(4, grad_t.at[:, pl.ds(0, SUB), :], grad_in.at[me])
-    drain(5, edge_back.at[0], edge_back_in.at[me])
-    drain(6, back_rows.at[0], back_in.at[:, pl.ds(0, SUB), :])
-    drain(7, edge_back_all.at[me], edge_back_all.at[me])
+    drain(0, rows_in.at[most])
+    drain(1, edge_in.at[most])
+    drain(2, chunk.at[most])
+    drain(3, edge_all.at[most])
+    drain(4, grad_in.at[pl.ds(0, chips - 1)])
+    drain(5, edge_back_in.at[most])
+    drain(6, back_in.at[:, pl.ds(0, h - SUB), :])
+    drain(7, edge_back_all.at[most])
+    drain(8, pair_in)
 
 
 def closing(n, sources, result, wave, loss_hbm, grad_hbm, group_hbm, loss, group, out, out_sem):
@@ -571,17 +604,20 @@
         vmem(2, h, rows), vmem(devices, 1, LANES), vmem(devices, 2, SUB, rows), vmem(devices, 1, LANES),
         vmem(devices, 4, SUB, h), vmem(devices, 1, LANES), vmem(h + SUB, 2 * h), vmem(4, 2, h, h),
         vmem(4, 2, h, h), vmem(sources, 2 * rows, coarse), vmem(rows, coarse), vmem(rows, coarse),
-        vmem(4, 2, h, h), vmem(4, h, h), vmem(devices, 1, LANES), vmem(devices, 4, SUB, h),
+        vmem(4, 2, h, h), vmem(4, devices // 2, 2, SUB, h), vmem(devices, 1, LANES), vmem(devices // 2, 4, SUB, h),
         vmem(devices, 1, LANES), vmem(devices, 1, LANES), vmem(devices, 2, SUB, rows), vmem(2, h, rows),
         pltpu.VMEM((8, 2, 2 * h, coarse), BF16), pltpu.VMEM((8, 2, 2 * rows, 2 * h), BF16),
         pltpu.VMEM((8, 2, 2 * rows, coarse), BF16), pltpu.VMEM((8, 2 * rows, coarse), BF16),
         vmem(sources, SUB, LANES),
         pltpu.SMEM((2, sources), jnp.int32), pltpu.SMEM((sources,), jnp.int32), pltpu.SMEM((NG,), F32),
         pltpu.SMEM((1,), jnp.int32),
-        pltpu.SemaphoreType.DMA((16,)),
-        pltpu.SemaphoreType.DMA((8, devices)), pltpu.SemaphoreType.DMA((8, devices)),
+        vmem(4, devices // 2, SUB, h), vmem(devices // 2, 4, SUB, h),
+        pltpu.VMEM((2, n, coarse), BF16), pltpu.VMEM((2, rows, n), BF16),
+        pltpu.SemaphoreType.DMA((24,)),
+        pltpu.SemaphoreType.DMA((9,)), pltpu.SemaphoreType.DMA((9,)), pltpu.SemaphoreType.DMA((devices // 2,)),
     ]
     arrays = [jnp.asarray(consts[k]) for k in NAMES]
+    hold = lambda value: pltpu.with_memory_space_constraint(value, pltpu.HBM)
     inside = pl.BlockSpec(memory_space=pltpu.VMEM)
     (result,) = pl.pallas_call(
         functools.partial(kernel, devices, n),
@@ -592,9 +628,10 @@
         out_specs=(inside,),
         scratch_shapes=scratch,
         compiler_params=pltpu.CompilerParams(
-            collective_id=0, has_side_effects=True, vmem_limit_bytes=58 * 1024 * 1024
+            collective_id=0, has_side_effects=True, vmem_limit_bytes=53 * 1024 * 1024
         ),
-    )(source_points.T, source_groups, group_logits, pupil_radius, mask_field, target_print, *arrays)
+    )(*map(hold, (source_points.T, source_groups, group_logits)), pupil_radius,
+      *map(hold, (mask_field, target_print, *arrays)))
     return pl.pallas_call(
         functools.partial(closing, n, sources),
         out_shape=(

time: 63.9 us -> 51.2 us (0.80)
  Pallas kernels: 61.5 us -> 49.8 us
  local copies, waits for them, and re-layouts: 0.95 us -> 0.01 us
    pallas_call x1, Pallas kernels: 60.1 us -> 48.4 us  [fused(): pl.pallas_call(functools.partial(kernel, devices, n), out_shape=(jax.Shap...]
    unnamed x4 -> x2, local copies, waits for them, and re-layouts: 0.95 us -> 0.01 us
where the time goes in v3:
time: 51.2 us; the launch traced here: 51.1 us
  Pallas kernels  49.8 us (97%)
  between operations  1.3 us (3%)
    pallas_call x1, Pallas kernels, fused(): pl.pallas_call(functools.partial(kernel, devices, n), out_shape=(jax.Shap...  48.4 us
    pallas_call x1, Pallas kernels, fused(): pl.pallas_call(functools.partial(closing, n, sources), out_shape=(jax.Sha...  1.39 us

profile of v3, /device:TPU:0, one launch (start us, length us, event | category | flops | bytes accessed | tf_op | source)
XLA Modules:
  0.0 51.1 jit_solution(15928099171985402114)
XLA Ops:
  1.3 0.0 copy-start
  1.3 48.4 %shard_map.175.result = f32[128,512]{1,0:T(8,128)S(1)} custom-call(s32[2,16]{1,0:T(2,128)} %bitcast.1, s32[16]{0:T(128)} %refs_1_.1, f32[8]{0:T(128)} %refs_2_.1, s32[1]{0:T(128)S(6)} %copy.19.refs_3_, f32[128,2048]{1,0:T(8,128)} %refs_4_.1, s32[128,2048]{1,0:T(8,128)} %refs_5_.1, bf16[2,256,2048]{2,1,0:T(8,128)(2,1)} %constant.20.clone.refs_6_.wave, ...), custom_call_target="tpu_custom_call" | custom-call | tf_op jit(solution)/shard_map/pallas_call | solution.py:622
  49.7 0.0 copy-done
  49.7 1.4 %shard_map.176 = (f32[1]{0:T(128)}, f32[128,2048]{1,0:T(8,128)}, f32[8]{0:T(128)}) custom-call(f32[128,512]{1,0:T(8,128)S(1)} %shard_map.175.result, bf16[2,256,2048]{2,1,0:T(8,128)(2,1)S(1)} %copy-done), custom_call_target="tpu_custom_call" | custom-call | tf_op jit(solution)/shard_map/pallas_call | solution.py:635
Async XLA Ops:
  1.3 48.4 %copy-start = (bf16[2,256,2048]{2,1,0:T(8,128)(2,1)S(1)}, bf16[2,256,2048]{2,1,0:T(8,128)(2,1)}, u32[]{:S(2)}) copy-start(bf16[2,256,2048]{2,1,0:T(8,128)(2,1)} %constant.20.clone.refs_6_.wave) | copy-start | bytes 6291460

commit v4 on v3

--- a/solution.py
+++ b/solution.py
@@ -57,8 +57,13 @@
     wave_x = np.concatenate([np.cos(wave_x), np.sin(wave_x)], 1)
     half_x = angles(near, 2 * freq + 1, 2 * n)
     half_x = np.concatenate([np.cos(half_x), -np.sin(half_x)], 1)
-    half_y = angles(2 * freq + 1, step * np.arange(coarse), 2 * n)
-    half_y = np.concatenate([np.cos(half_y), np.sin(half_y)], 0)
+    spots = step * np.arange(coarse // 2) + step // 2
+    half_y = angles(2 * freq + 1, spots, 2 * n)
+    half_y = [halves(np.cos(half_y)), halves(np.sin(half_y))]
+    ahead = np.stack([np.concatenate([t[0], t[0], t[1]], 0) for t in half_y])
+    behind = np.stack([
+        np.block([[t[0].T, t[1].T], [t[0].T, np.zeros_like(t[0].T)]]) for t in half_y
+    ])
     far = angles(rows * np.arange(devices), freq, n)
     far = np.stack([np.cos(far), np.sin(far)])[:, :, None, :].astype(np.float32)
     half_far = angles(rows * np.arange(devices), 2 * freq + 1, 2 * n)
@@ -66,7 +71,9 @@
     half_far = half_far[:, :, None, :].astype(np.float32)
     block = 2 * LANES
     extra = n // step - block // step
-    lag = np.mod(np.arange(block)[None, :] - step * (np.arange(coarse + extra) - extra)[:, None], n)
+    index = np.arange(coarse // 2 + extra)[:, None]
+    spot = np.concatenate([step * (index - extra) + step // 2, -step * index - step // 2], 0)
+    lag = np.mod(np.arange(block)[None, :] - spot, n)
     kernel = np.ones(n)
     for f in range(1, K):
         kernel += 2.0 * np.cos(2.0 * math.pi * np.mod(f * np.arange(n), n) / n)
@@ -79,8 +86,8 @@
         "wave_x": halves(wave_x),
         "half_x": halves(half_x),
         "half_xt": np.concatenate(list(halves(half_x.T)[[0, 0, 1]]), 1),
-        "half_y": halves(half_y),
-        "half_yt": halves(half_y.T),
+        "half_y": ahead,
+        "half_yt": behind,
         "up": halves(up),
         "far": far,
         "half_far": half_far,
@@ -154,13 +161,28 @@
             recv_sem=recv_sem.at[phase] if sem is None else sem, device_id={"slab": peer},
         )
 
+    group = 4
+    planes = devices // group
+    lower = 1 - me // (group * (planes // 2))
+
+    def plane_of(i):
+        return lower * (planes - 1 - 2 * i) + i
+
     def send_all(phase, src_of, dst):
-        def body(i, carry):
-            peer = lax.rem(me + i, devices)
-            copy_to(phase, peer, src_of(peer), dst).start()
-            return carry
-
-        lax.fori_loop(1, devices, body, 0)
+        for i in range(devices):
+            peer = plane_of(i // group) * group + lax.rem(me + i % group, group)
+
+            @pl.when(peer != me)
+            def _():
+                copy_to(phase, peer, src_of(peer), dst).start()
+
+    def each_chip(act, reverse=False):
+        for i in range(chips)[:: -1 if reverse else 1]:
+            other = plane_of(i // 2) * 2 + lax.rem(chip + i % 2, 2)
+
+            @pl.when(other != chip)
+            def _():
+                act(other * 2 + core)
 
     def wait_all(phase, ref, sem=None):
         copy_to(phase, partner, ref, ref, sem).wait_recv()
@@ -219,8 +241,8 @@
         edge_out[i] = jnp.zeros((1, LANES), F32)
 
     pl.semaphore_wait(barrier, devices - 1)
+    send_all(1, lambda p: edge_out.at[p], edge_in.at[me])
     send_all(0, lambda p: rows_t.at[:, pl.ds(p * SUB, SUB), :], rows_in.at[me])
-    send_all(1, lambda p: edge_out.at[p], edge_in.at[me])
     rows_in[me] = rows_t[:, pl.ds(me * SUB, SUB), :]
     edge_in[me] = edge_out[me]
 
@@ -237,11 +259,19 @@
 
     loads["up"].wait()
     extra = (n - block) // step
+
+    def taps(b):
+        first, second = extra - b * (block // step), extra + 2 * h + b * (block // step)
+        return slice(first, first + 2 * h), slice(second, second + 2 * h)
+
     for b in range(blocks):
-        start = extra - b * (block // step)
         for part in range(2):
-            up_t[part, b * block : (b + 1) * block, :] = tab["up"][part, start : start + coarse, :].T
-
+            for side, spot in enumerate(taps(b)):
+                up_t[part, b * block : (b + 1) * block, side * 2 * h : (side + 1) * 2 * h] = tab["up"][part, spot, :].T
+
+    wait_all(1, edge_in.at[most])
+    edge_all[me] = jnp.sum(edge_in[...], 0)
+    send_all(3, lambda p: edge_all.at[me], edge_all.at[me])
     wait_all(0, rows_in.at[most])
     gathered = rows_in[...].reshape(devices * 2 * SUB, rows)
     turned = product(split(gathered), both("wave_x")).reshape(devices, 2 * SUB, 2 * h)
@@ -252,15 +282,8 @@
     for i, value in enumerate(mixes(sum_c[:SUB], sum_c[SUB:], sum_s[:SUB], sum_s[SUB:])):
         chunk[me, i] = value
 
-    def share(i, carry):
-        copy_to(2, lax.rem(me + 2 * i, devices), chunk.at[me], chunk.at[me], near_sem.at[chip]).start()
-        return carry
-
-    lax.fori_loop(1, chips, share, 0)
+    each_chip(lambda peer: copy_to(2, peer, chunk.at[me], chunk.at[me], near_sem.at[chip]).start())
     copy_to(2, partner, chunk.at[me], chunk.at[me]).start()
-    wait_all(1, edge_in.at[most])
-    edge_all[me] = jnp.sum(edge_in[...], 0)
-    send_all(3, lambda p: edge_all.at[me], edge_all.at[me])
 
     loads["half_far"].wait()
     loads["half_x"].wait()
@@ -269,13 +292,11 @@
     turn_s = column(tab["half_far"][1, me])
 
 
-    def relay(i, carry):
-        peer = lax.rem(me + 2 * i, devices)
+    def relay(peer):
         wait_all(2, chunk.at[peer], near_sem.at[peer // 2])
         copy_to(2, partner, chunk.at[peer], chunk.at[peer]).start()
-        return carry
-
-    lax.fori_loop(1, chips, relay, 0)
+
+    each_chip(relay, reverse=True)
     wait_all(2, chunk.at[pl.ds(0, chips)])
     wait_all(3, edge_all.at[most])
     shifted = []
@@ -359,16 +380,31 @@
             keep(dest, low_where, quarter[0], op + om)
             keep(dest, low_where, quarter[3], op - om)
 
+    dims = (((1,), (0,)), ((), ()))
+
+    def once(left, right):
+        return lax.dot_general(left, right, dims, preferred_element_type=F32)
+
     def to_rows(slot):
         wide = product(both("half_x"), (folded[slot, 0], folded[slot, 1]))
-        keep(wides.at[slot], slice(0, rows), slice(None), wide[:, : 2 * h])
-        keep(wides.at[slot], slice(rows, 2 * rows), slice(None), wide[:, 2 * h :])
+        for part in range(2):
+            for side in range(2):
+                high, low = split(wide[:, quarter[2 * part + side]])
+                wides[slot, side, part * rows : (part + 1) * rows, :h] = high
+                wides[slot, side, part * rows : (part + 1) * rows, h:] = low
 
     def to_field(s, slot):
-        field = product((wides[slot, 0], wides[slot, 1]), both("half_y"))
-        fields[s] = field
-        re, im = field[:rows], field[rows:]
-        image[...] += share_of(s) * (re * re + im * im)
+        even, odd = (
+            once(wides[slot, side], tab["half_y"][side, : 2 * h])
+            + once(wides[slot, side, :, :h], tab["half_y"][side, 2 * h :])
+            for side in range(2)
+        )
+        weight = share_of(s)
+        for side, field in enumerate((even + odd, even - odd)):
+            where = slice(side * 2 * h, (side + 1) * 2 * h)
+            fields[s, :, where] = field
+            re, im = field[:rows], field[rows:]
+            image[:, where] += weight * (re * re + im * im)
 
     def forward(i, carry):
         base = i * unroll
@@ -387,9 +423,8 @@
     squares = jnp.zeros((rows, LANES), F32)
     image_pair = split(image[...])
     for b in range(blocks):
-        start = extra - b * (block // step)
         where = slice(b * block, (b + 1) * block)
-        up = (tab["up"][0, start : start + coarse, :], tab["up"][1, start : start + coarse, :])
+        up = [jnp.concatenate([tab["up"][part, spot, :] for spot in taps(b)], 0) for part in range(2)]
         intensity = product(image_pair, up)
         resist = 1.0 / (1.0 + jnp.exp(-steepness * (intensity - threshold)))
         misfit = resist - target[:, where].astype(F32)
@@ -414,21 +449,27 @@
             weak, re, im = pull[where, :], fields[s, where, :], fields[s, other, :]
             down_r, down_i = weak * re, weak * im
             total = total + (down_r * re + down_i * im)
-            keep(dest, where, slice(None), down_r)
-            keep(dest, other, slice(None), down_i)
+            for spot, value in ((where, down_r), (other, down_i)):
+                first, second = value[:, : 2 * h], value[:, 2 * h :]
+                for side, pair in enumerate((first + second, first - second)):
+                    high, low = split(pair)
+                    dest[side, spot, : 2 * h] = high
+                    dest[side, spot, 2 * h :] = low
         total = total[:SUB] + total[SUB:]
         totals[s] = total[:, :h] + total[:, h : 2 * h] + total[:, 2 * h : 3 * h] + total[:, 3 * h :]
 
     def from_field(s, slot):
-        settle = product((weighed[slot, 0], weighed[slot, 1]), both("half_yt")) * (2.0 * share_of(s))
-        for part in range(2):
-            high, low = split(settle[part * rows : (part + 1) * rows])
-            settled[slot, :rows, part * 2 * h : (part + 1) * 2 * h] = high
-            settled[slot, rows:, part * 2 * h : (part + 1) * 2 * h] = low
+        weight = 2.0 * share_of(s)
+        for side in range(2):
+            settle = once(weighed[slot, side], tab["half_yt"][side])
+            settle = (settle[:, :h] + settle[:, h:]) * weight
+            for part in range(2):
+                high, low = split(settle[part * rows : (part + 1) * rows])
+                settled[slot, :rows, quarter[2 * part + side]] = high
+                settled[slot, rows:, quarter[2 * part + side]] = low
 
     def from_rows(s, slot):
         kept = masks(s)
-        dims = (((1,), (0,)), ((), ()))
         full = lax.dot_general(half_xt[:, : 2 * rows], settled[slot], dims, preferred_element_type=F32)
         full = full + lax.dot_general(
             half_xt[:, 2 * rows :], settled[slot, :rows], dims, preferred_element_type=F32
@@ -498,13 +539,11 @@
     for i in range(4):
         pair_sum[:, i] = grad_t[i, :, core] + pair_in[i]
 
-    def hand_over(i, carry):
-        peer = lax.rem(me + 2 * i, devices)
-        copy_to(4, peer, pair_sum.at[peer // 2], grad_in.at[chip]).start()
-        return carry
-
-    lax.fori_loop(1, chips, hand_over, 0)
+    each_chip(lambda peer: copy_to(4, peer, pair_sum.at[peer // 2], grad_in.at[chip]).start())
     grad_in[chip] = pair_sum[chip]
+    wait_all(5, edge_back_in.at[most])
+    edge_back_all[me] = jnp.sum(edge_back_in[...], 0)
+    send_all(7, lambda p: edge_back_all.at[me], edge_back_all.at[me])
     wait_all(4, grad_in.at[pl.ds(0, chips - 1)])
 
     def unmix(u, v, wp, wm):
@@ -521,9 +560,6 @@
     back_rows[...] = gathered.reshape(devices, 2, SUB, rows)
     send_all(6, lambda p: back_rows.at[p], back_in.at[:, pl.ds(me * SUB, SUB), :])
     back_in[:, pl.ds(me * SUB, SUB), :] = back_rows[me]
-    wait_all(5, edge_back_in.at[most])
-    edge_back_all[me] = jnp.sum(edge_back_in[...], 0)
-    send_all(7, lambda p: edge_back_all.at[me], edge_back_all.at[me])
     wait_all(7, edge_back_all.at[most])
 
     sums = edge_back_all[9]
@@ -774,7 +810,7 @@
 
 
 def on_device(devices, mask_field, *others):
-    tiles = mask_field.shape[0] == LANES and K // 2 == LANES == SUB * devices and devices >= 10
+    tiles = mask_field.shape[0] == LANES and K // 2 == LANES == SUB * devices and devices % 8 == 0 and devices >= 10
     return (fused if tiles else plain)(devices, mask_field, *others)
 
 

time: 51.2 us -> 48 us (0.938)
  Pallas kernels: 49.8 us -> 46.5 us
    pallas_call x1, Pallas kernels: 48.4 us -> 45.1 us  [fused(): pl.pallas_call(functools.partial(kernel, devices, n), out_shape=(jax.Shap...]
where the time goes in v4:
time: 48 us; the launch traced here: 47.8 us
  Pallas kernels  46.5 us (97%)
  between operations  1.3 us (3%)
    pallas_call x1, Pallas kernels, fused(): pl.pallas_call(functools.partial(kernel, devices, n), out_shape=(jax.Shap...  45.1 us
    pallas_call x1, Pallas kernels, fused(): pl.pallas_call(functools.partial(closing, n, sources), out_shape=(jax.Sha...  1.39 us

profile of v4, /device:TPU:0, one launch (start us, length us, event | category | flops | bytes accessed | tf_op | source)
XLA Modules:
  0.0 47.8 jit_solution(5921516845770319018)
XLA Ops:
  1.3 0.0 copy-start
  1.3 45.1 %shard_map.175.result = f32[128,512]{1,0:T(8,128)S(1)} custom-call(s32[2,16]{1,0:T(2,128)} %bitcast.1, s32[16]{0:T(128)} %refs_1_.1, f32[8]{0:T(128)} %refs_2_.1, s32[1]{0:T(128)S(6)} %copy.19.refs_3_, f32[128,2048]{1,0:T(8,128)} %refs_4_.1, s32[128,2048]{1,0:T(8,128)} %refs_5_.1, bf16[2,256,2048]{2,1,0:T(8,128)(2,1)} %constant.20.clone.refs_6_.wave, ...), custom_call_target="tpu_custom_call" | custom-call | tf_op jit(solution)/shard_map/pallas_call | solution.py:658
  46.4 0.0 copy-done
  46.4 1.4 %shard_map.176 = (f32[1]{0:T(128)}, f32[128,2048]{1,0:T(8,128)}, f32[8]{0:T(128)}) custom-call(f32[128,512]{1,0:T(8,128)S(1)} %shard_map.175.result, bf16[2,256,2048]{2,1,0:T(8,128)(2,1)S(1)} %copy-done), custom_call_target="tpu_custom_call" | custom-call | tf_op jit(solution)/shard_map/pallas_call | solution.py:671
Async XLA Ops:
  1.3 45.1 %copy-start = (bf16[2,256,2048]{2,1,0:T(8,128)(2,1)S(1)}, bf16[2,256,2048]{2,1,0:T(8,128)(2,1)}, u32[]{:S(2)}) copy-start(bf16[2,256,2048]{2,1,0:T(8,128)(2,1)} %constant.20.clone.refs_6_.wave) | copy-start | bytes 6291460

commit v5 on v4

--- a/solution.py
+++ b/solution.py
@@ -51,7 +51,7 @@
     step = n // coarse
     freq = np.arange(h)
     near = np.arange(rows)
-    wave_y = angles(freq, np.arange(n), n)
+    wave_y = angles(freq, np.arange(n // 2), n)
     wave_y = np.concatenate([np.cos(wave_y), np.sin(wave_y)], 0)
     wave_x = angles(near, freq, n)
     wave_x = np.concatenate([np.cos(wave_x), np.sin(wave_x)], 1)
@@ -106,9 +106,9 @@
     refs = refs[1:]
     tab = dict(zip(NAMES, refs[: len(NAMES)]))
     refs = refs[len(NAMES) :]
-    (mask, target, rows_t, edge_out, rows_in, edge_in, chunk, edge_all, ext, band, data, fields, image, pull,
+    (mask, target, rows_t, edge_out, rows_in, edge_in, chunk, edge_all, exts, band, data, fields, image, pull,
      grads, grad_t, edge_back, grad_in, edge_back_in, edge_back_all, back_rows, back_in,
-     folded, wides, weighed, settled, totals, points, groups, logits, radius,
+     folded, wides, weighed, settled, totals, keeps, points, groups, logits, radius,
      pair_in, pair_sum, up_t, slopes, local_sem, send_sem, recv_sem, near_sem) = refs
     h = K // 2
     coarse = 2 * K
@@ -126,13 +126,15 @@
 
     loads = {}
     small = (points, groups, logits, radius)
-    pieces = [slice(c, c + n // 4) for c in range(0, n, n // 4)]
+    part = n // 8
+    pieces = [(slice(c, c + part), slice(c + n // 2, c + n // 2 + part)) for c in range(0, n // 2, part)]
     for i, (name, src, dst) in enumerate(
         [
             piece
-            for k, where in enumerate(pieces)
+            for k, (where, away) in enumerate(pieces)
             for piece in (
-                (f"mask{k}", mask_hbm.at[:, where], mask.at[:, where]),
+                (f"near{k}", mask_hbm.at[:, where], mask.at[:, where]),
+                (f"away{k}", mask_hbm.at[:, away], mask.at[:, away]),
                 (f"wave_y{k}", sources_in["wave_y"].at[:, :, where], tab["wave_y"].at[:, :, where]),
             )
         ]
@@ -195,12 +197,16 @@
     def column(row):
         return jnp.broadcast_to(row, (LANES, LANES)).T
 
-    transformed = 0.0
-    for k, where in enumerate(pieces):
-        loads[f"mask{k}"].wait()
-        loads[f"wave_y{k}"].wait()
+    even = odd = 0.0
+    for k, (where, away) in enumerate(pieces):
+        for name in ("near", "away", "wave_y"):
+            loads[f"{name}{k}"].wait()
         wave = (tab["wave_y"][0, :, where], tab["wave_y"][1, :, where])
-        transformed = transformed + product(split(mask[:, where]), wave, flip=True)
+        first, second = mask[:, where], mask[:, away]
+        even = even + product(split(first + second), wave, flip=True)
+        odd = odd + product(split(first - second), wave, flip=True)
+    wide_lane = lax.broadcasted_iota(jnp.int32, (rows, 2 * h), 1)
+    transformed = jnp.where(lax.rem(wide_lane, 2) == 0, even, odd)
     rows_t[0] = transformed[:, :h].T
     rows_t[1] = transformed[:, h:].T
     loads["edge"].wait()
@@ -268,6 +274,34 @@
         for part in range(2):
             for side, spot in enumerate(taps(b)):
                 up_t[part, b * block : (b + 1) * block, side * 2 * h : (side + 1) * 2 * h] = tab["up"][part, spot, :].T
+    cutoff = radius[0]
+    limit = (cutoff * cutoff).astype(F32)
+    lane_index = lane.astype(F32)
+    chunk_rows = [slice(c, c + 2 * SUB) for c in range(0, h, 2 * SUB)]
+    row_index = lax.broadcasted_iota(jnp.int32, (2 * SUB, LANES), 0).astype(F32)
+
+    def masks(s):
+        first = ((points[0, s] - GRID // 2) * cutoff // shift_scale).astype(F32)
+        second = ((points[1, s] - GRID // 2) * cutoff // shift_scale).astype(F32)
+        col_p, col_m = lane_index + second, second - 1.0 - lane_index
+        col_p, col_m = col_p * col_p, col_m * col_m
+
+        def of(where):
+            row_p = row_index + (first + where.start)
+            row_m = (first - 1.0 - where.start) - row_index
+            room_p, room_m = limit - row_p * row_p, limit - row_m * row_m
+            return col_p <= room_p, col_m <= room_p, col_p <= room_m, col_m <= room_m
+
+        return of
+
+    def fill(s, carry):
+        kept = masks(s)
+        for where in chunk_rows:
+            for q, flag in enumerate(kept(where)):
+                keeps[s, q, where, :] = jnp.where(flag, 1.0, 0.0)
+        return carry
+
+    lax.fori_loop(0, sources, fill, 0)
 
     wait_all(1, edge_in.at[most])
     edge_all[me] = jnp.sum(edge_in[...], 0)
@@ -302,6 +336,7 @@
     shifted = []
     plain = []
     for i in range(4):
+        ext = exts.at[i]
         ext[:h, :h] = chunk[:, i].reshape(h, h).T
         ext[h : h + 1, :h] = edge_all[i]
         ext[:h, h:] = column(edge_all[4 + i])
@@ -329,26 +364,6 @@
     turn(2, data[1, 1], data[3, 1], -1)
     turn(3, data[0, 1], data[2, 1], -1)
 
-    cutoff = radius[0]
-    limit = (cutoff * cutoff).astype(F32)
-    lane_index = lane.astype(F32)
-    chunk_rows = [slice(c, c + 2 * SUB) for c in range(0, h, 2 * SUB)]
-    row_index = lax.broadcasted_iota(jnp.int32, (2 * SUB, LANES), 0).astype(F32)
-
-    def masks(s):
-        first = ((points[0, s] - GRID // 2) * cutoff // shift_scale).astype(F32)
-        second = ((points[1, s] - GRID // 2) * cutoff // shift_scale).astype(F32)
-        col_p, col_m = lane_index + second, second - 1.0 - lane_index
-        col_p, col_m = col_p * col_p, col_m * col_m
-
-        def of(where):
-            row_p = row_index + (first + where.start)
-            row_m = (first - 1.0 - where.start) - row_index
-            room_p, room_m = limit - row_p * row_p, limit - row_m * row_m
-            return col_p <= room_p, col_m <= room_p, col_p <= room_m, col_m <= room_m
-
-        return of
-
     def share_of(s):
         return lane_sum(jnp.where(lane == s, share_row, 0.0))
 
@@ -362,23 +377,20 @@
     image[...] = jnp.zeros_like(image)
 
     def mask_band(s, slot):
-        kept = masks(s)
         dest = folded.at[slot]
         for where in chunk_rows:
-            keeps = kept(where)
+            kept = [keeps[s, q, where, :] for q in range(4)]
             low_where = slice(where.start + h, where.stop + h)
-            pp, pm, mp, mm = (jnp.where(keeps[q], band[q, 0, where, :], 0.0) for q in range(4))
-            ep, em, op, om = pp + mp, pm + mm, mp - pp, mm - pm
-            keep(dest, where, quarter[0], ep + em)
-            keep(dest, where, quarter[3], ep - em)
-            keep(dest, low_where, quarter[1], om - op)
-            keep(dest, low_where, quarter[2], op + om)
-            pp, pm, mp, mm = (jnp.where(keeps[q], band[q, 1, where, :], 0.0) for q in range(4))
-            ep, em, op, om = pp + mp, pm + mm, pp - mp, pm - mm
-            keep(dest, where, quarter[1], em - ep)
-            keep(dest, where, quarter[2], ep + em)
-            keep(dest, low_where, quarter[0], op + om)
-            keep(dest, low_where, quarter[3], op - om)
+            pp, pm, mp, mm = (kept[q] * band[q, 0, where, :] for q in range(4))
+            keep(dest, where, quarter[0], pp + mp)
+            keep(dest, where, quarter[1], pm + mm)
+            keep(dest, low_where, quarter[2], mp - pp)
+            keep(dest, low_where, quarter[3], mm - pm)
+            pp, pm, mp, mm = (kept[q] * band[q, 1, where, :] for q in range(4))
+            keep(dest, where, quarter[2], pp + mp)
+            keep(dest, where, quarter[3], pm + mm)
+            keep(dest, low_where, quarter[0], pp - mp)
+            keep(dest, low_where, quarter[1], pm - mm)
 
     dims = (((1,), (0,)), ((), ()))
 
@@ -387,9 +399,10 @@
 
     def to_rows(slot):
         wide = product(both("half_x"), (folded[slot, 0], folded[slot, 1]))
-        for part in range(2):
-            for side in range(2):
-                high, low = split(wide[:, quarter[2 * part + side]])
+        p_r, m_r, p_i, m_i = (wide[:, q] for q in quarter)
+        for part, sides in enumerate(((p_r + m_r, m_i - p_i), (p_i + m_i, p_r - m_r))):
+            for side, value in enumerate(sides):
+                high, low = split(value)
                 wides[slot, side, part * rows : (part + 1) * rows, :h] = high
                 wides[slot, side, part * rows : (part + 1) * rows, h:] = low
 
@@ -460,31 +473,32 @@
 
     def from_field(s, slot):
         weight = 2.0 * share_of(s)
+        sides = []
         for side in range(2):
             settle = once(weighed[slot, side], tab["half_yt"][side])
-            settle = (settle[:, :h] + settle[:, h:]) * weight
-            for part in range(2):
-                high, low = split(settle[part * rows : (part + 1) * rows])
-                settled[slot, :rows, quarter[2 * part + side]] = high
-                settled[slot, rows:, quarter[2 * part + side]] = low
+            sides.append((settle[:, :h] + settle[:, h:]) * weight)
+        even_r, even_i, odd_i, odd_r = (side[part * rows : (part + 1) * rows] for side in sides for part in range(2))
+        for q, value in enumerate((even_r + odd_r, even_r - odd_r, even_i - odd_i, even_i + odd_i)):
+            high, low = split(value)
+            settled[slot, :rows, quarter[q]] = high
+            settled[slot, rows:, quarter[q]] = low
 
     def from_rows(s, slot):
-        kept = masks(s)
         full = lax.dot_general(half_xt[:, : 2 * rows], settled[slot], dims, preferred_element_type=F32)
         full = full + lax.dot_general(
             half_xt[:, 2 * rows :], settled[slot, :rows], dims, preferred_element_type=F32
         )
         for where in chunk_rows:
-            keeps = kept(where)
+            kept = [keeps[s, q, where, :] for q in range(4)]
             top, low = full[where], full[where.start + h : where.stop + h]
-            ee_r, no_i, ee_i, eo_r = (top[:, q] for q in quarter)
-            oe_i, oo_r, ne_r, oo_i = (low[:, q] for q in quarter)
-            ep, em, op, om = ee_r + eo_r, ee_r - eo_r, oo_r - ne_r, -ne_r - oo_r
-            for q, value in enumerate((ep + op, em + om, ep - op, em - om)):
-                grads[q, 0, where, :] += jnp.where(keeps[q], value, 0.0)
-            ep, em, op, om = ee_i - no_i, ee_i + no_i, oe_i + oo_i, oe_i - oo_i
-            for q, value in enumerate((ep + op, em + om, ep - op, em - om)):
-                grads[q, 1, where, :] += jnp.where(keeps[q], value, 0.0)
+            sums_of = [top[:, q] for q in quarter]
+            turns_of = [low[:, q] for q in quarter]
+            for part in range(2):
+                for side in range(2):
+                    even, odd = sums_of[2 * part + side], turns_of[2 - 2 * part + side]
+                    more, less = (even - odd, even + odd) if part == 0 else (even + odd, even - odd)
+                    grads[side, part, where, :] += kept[side] * more
+                    grads[2 + side, part, where, :] += kept[2 + side] * less
 
     def backward(i, carry):
         base = i * unroll
@@ -512,7 +526,8 @@
     pieces = ((pp[0], mm[0]), (pm[0], mp[0]), (-pp[1], mm[1]), (-pm[1], mp[1]))
     last_row = jnp.zeros((1, LANES), F32)
     for i, (first, second) in enumerate(pieces):
-        ext[...] = jnp.zeros_like(ext)
+        ext = exts.at[i]
+        ext[...] = jnp.zeros((h + SUB, 2 * h), F32)
         if i in (0, 2):
             ext[1 : h + 1, :h] = second
             moved = pltpu.roll(ext[...], 1, 1)
@@ -615,12 +630,16 @@
     ]
     for store in stores:
         store.start()
-    pair = split(result[:, : 2 * h])
+    value = result[:, : 2 * h]
+    turn = lax.rem(lax.broadcasted_iota(jnp.int32, value.shape, 1), 2) == 0
+    pairs = split(value), split(jnp.where(turn, value, -value))
     spread = result[:, 2 * h : 2 * h + LANES]
     adds = jnp.concatenate([spread, spread], 1)
     for b in range(blocks):
         where = slice(b * block, (b + 1) * block)
-        out[:, where] = product(pair, (wave[0, :, where], wave[1, :, where])) + adds
+        side, start = divmod(b * block, n // 2)
+        from_where = slice(start, start + block)
+        out[:, where] = product(pairs[side], (wave[0, :, from_where], wave[1, :, from_where])) + adds
         stores.append(pltpu.make_async_copy(out.at[:, where], grad_hbm.at[:, where], out_sem.at[b]))
         stores[-1].start()
     for store in stores:
@@ -638,18 +657,18 @@
     scratch = [pltpu.VMEM(consts[k].shape, consts[k].dtype) for k in NAMES] + [
         vmem(rows, n), pltpu.VMEM((rows, n), jnp.int32),
         vmem(2, h, rows), vmem(devices, 1, LANES), vmem(devices, 2, SUB, rows), vmem(devices, 1, LANES),
-        vmem(devices, 4, SUB, h), vmem(devices, 1, LANES), vmem(h + SUB, 2 * h), vmem(4, 2, h, h),
+        vmem(devices, 4, SUB, h), vmem(devices, 1, LANES), vmem(4, h + SUB, 2 * h), vmem(4, 2, h, h),
         vmem(4, 2, h, h), vmem(sources, 2 * rows, coarse), vmem(rows, coarse), vmem(rows, coarse),
         vmem(4, 2, h, h), vmem(4, devices // 2, 2, SUB, h), vmem(devices, 1, LANES), vmem(devices // 2, 4, SUB, h),
         vmem(devices, 1, LANES), vmem(devices, 1, LANES), vmem(devices, 2, SUB, rows), vmem(2, h, rows),
         pltpu.VMEM((8, 2, 2 * h, coarse), BF16), pltpu.VMEM((8, 2, 2 * rows, 2 * h), BF16),
         pltpu.VMEM((8, 2, 2 * rows, coarse), BF16), pltpu.VMEM((8, 2 * rows, coarse), BF16),
-        vmem(sources, SUB, LANES),
+        vmem(sources, SUB, LANES), vmem(sources, 4, h, h),
         pltpu.SMEM((2, sources), jnp.int32), pltpu.SMEM((sources,), jnp.int32), pltpu.SMEM((NG,), F32),
         pltpu.SMEM((1,), jnp.int32),
         vmem(4, devices // 2, SUB, h), vmem(devices // 2, 4, SUB, h),
         pltpu.VMEM((2, n, coarse), BF16), pltpu.VMEM((2, rows, n), BF16),
-        pltpu.SemaphoreType.DMA((24,)),
+        pltpu.SemaphoreType.DMA((26,)),
         pltpu.SemaphoreType.DMA((9,)), pltpu.SemaphoreType.DMA((9,)), pltpu.SemaphoreType.DMA((devices // 2,)),
     ]
     arrays = [jnp.asarray(consts[k]) for k in NAMES]

time: 48 us -> 46.9 us (0.977)
  Pallas kernels: 46.5 us -> 45.4 us
    pallas_call x1, Pallas kernels: 45.1 us -> 44 us  [fused(): pl.pallas_call(functools.partial(kernel, devices, n), out_shape=(jax.Shap...]
where the time goes in v5:
time: 46.9 us; the launch traced here: 46.7 us
  Pallas kernels  45.4 us (97%)
  between operations  1.3 us (3%)
    pallas_call x1, Pallas kernels, fused(): pl.pallas_call(functools.partial(kernel, devices, n), out_shape=(jax.Shap...  44 us
    pallas_call x1, Pallas kernels, fused(): pl.pallas_call(functools.partial(closing, n, sources), out_shape=(jax.Sha...  1.39 us

profile of v5, /device:TPU:0, one launch (start us, length us, event | category | flops | bytes accessed | tf_op | source)
XLA Modules:
  0.0 46.7 jit_solution(17116172960490390842)
XLA Ops:
  1.3 0.0 copy-start
  1.3 44.0 %shard_map.175.result = f32[128,512]{1,0:T(8,128)S(1)} custom-call(s32[2,16]{1,0:T(2,128)} %bitcast.1, s32[16]{0:T(128)} %refs_1_.1, f32[8]{0:T(128)} %refs_2_.1, s32[1]{0:T(128)S(6)} %copy.19.refs_3_, f32[128,2048]{1,0:T(8,128)} %refs_4_.1, s32[128,2048]{1,0:T(8,128)} %refs_5_.1, bf16[2,256,1024]{2,1,0:T(8,128)(2,1)} %constant.20.clone.refs_6_.wave, ...), custom_call_target="tpu_custom_call" | custom-call | tf_op jit(solution)/shard_map/pallas_call | solution.py:677
  45.3 0.0 copy-done
  45.3 1.4 %shard_map.176 = (f32[1]{0:T(128)}, f32[128,2048]{1,0:T(8,128)}, f32[8]{0:T(128)}) custom-call(f32[128,512]{1,0:T(8,128)S(1)} %shard_map.175.result, bf16[2,256,1024]{2,1,0:T(8,128)(2,1)S(1)} %copy-done), custom_call_target="tpu_custom_call" | custom-call | tf_op jit(solution)/shard_map/pallas_call | solution.py:690
Async XLA Ops:
  1.3 44.0 %copy-start = (bf16[2,256,1024]{2,1,0:T(8,128)(2,1)S(1)}, bf16[2,256,1024]{2,1,0:T(8,128)(2,1)}, u32[]{:S(2)}) copy-start(bf16[2,256,1024]{2,1,0:T(8,128)(2,1)} %constant.20.clone.refs_6_.wave) | copy-start | bytes 3145732

commit v6 on v5

--- a/solution.py
+++ b/solution.py
@@ -126,6 +126,7 @@
 
     loads = {}
     small = (points, groups, logits, radius)
+    late = ("up", "half_far", "half_x", "half_y", "target", "half_yt", "half_xt")
     part = n // 8
     pieces = [(slice(c, c + part), slice(c + n // 2, c + n // 2 + part)) for c in range(0, n // 2, part)]
     for i, (name, src, dst) in enumerate(
@@ -144,7 +145,8 @@
         + [(k, sources_in[k], tab[k]) for k in ("half_yt", "half_xt")]
     ):
         loads[name] = pltpu.make_async_copy(src, dst, local_sem.at[i])
-        loads[name].start()
+        if name not in late:
+            loads[name].start()
 
     barrier = pltpu.get_barrier_semaphore()
 
@@ -205,6 +207,8 @@
         first, second = mask[:, where], mask[:, away]
         even = even + product(split(first + second), wave, flip=True)
         odd = odd + product(split(first - second), wave, flip=True)
+    for name in late:
+        loads[name].start()
     wide_lane = lax.broadcasted_iota(jnp.int32, (rows, 2 * h), 1)
     transformed = jnp.where(lax.rem(wide_lane, 2) == 0, even, odd)
     rows_t[0] = transformed[:, :h].T

time: 46.9 us -> 46.8 us (level)
  no operation moved by 1% of the time
where the time goes in v6:
time: 46.8 us; the launch traced here: 46.7 us
  Pallas kernels  45.4 us (97%)
  between operations  1.3 us (3%)
    pallas_call x1, Pallas kernels, fused(): pl.pallas_call(functools.partial(kernel, devices, n), out_shape=(jax.Shap...  44 us
    pallas_call x1, Pallas kernels, fused(): pl.pallas_call(functools.partial(closing, n, sources), out_shape=(jax.Sha...  1.4 us

profile of v6, /device:TPU:0, one launch (start us, length us, event | category | flops | bytes accessed | tf_op | source)
XLA Modules:
  0.0 46.7 jit_solution(7814748604063115267)
XLA Ops:
  1.3 0.0 copy-start
  1.3 44.0 %shard_map.175.result = f32[128,512]{1,0:T(8,128)S(1)} custom-call(s32[2,16]{1,0:T(2,128)} %bitcast.1, s32[16]{0:T(128)} %refs_1_.1, f32[8]{0:T(128)} %refs_2_.1, s32[1]{0:T(128)S(6)} %copy.19.refs_3_, f32[128,2048]{1,0:T(8,128)} %refs_4_.1, s32[128,2048]{1,0:T(8,128)} %refs_5_.1, bf16[2,256,1024]{2,1,0:T(8,128)(2,1)} %constant.20.clone.refs_6_.wave, ...), custom_call_target="tpu_custom_call" | custom-call | tf_op jit(solution)/shard_map/pallas_call | solution.py:681
  45.3 0.0 copy-done
  45.3 1.4 %shard_map.176 = (f32[1]{0:T(128)}, f32[128,2048]{1,0:T(8,128)}, f32[8]{0:T(128)}) custom-call(f32[128,512]{1,0:T(8,128)S(1)} %shard_map.175.result, bf16[2,256,1024]{2,1,0:T(8,128)(2,1)S(1)} %copy-done), custom_call_target="tpu_custom_call" | custom-call | tf_op jit(solution)/shard_map/pallas_call | solution.py:694
Async XLA Ops:
  1.3 44.0 %copy-start = (bf16[2,256,1024]{2,1,0:T(8,128)(2,1)S(1)}, bf16[2,256,1024]{2,1,0:T(8,128)(2,1)}, u32[]{:S(2)}) copy-start(bf16[2,256,1024]{2,1,0:T(8,128)(2,1)} %constant.20.clone.refs_6_.wave) | copy-start | bytes 3145732
